TPU v7x, 32 devices: a 4x4x1 block of a 4x4x8 slice. The times are simulated.
32 devices in a mesh: pod: 1 (over z), data: 4 (over y), tensor: 8 (over x, core).
Axes of the slice: x: 4, y: 4, z: 1, core: 2. Of those that a mesh axis runs over, the one named last changes fastest.
The devices are a block of a 4x4x8 slice.
Arguments:
- token_ids: int32 [32768], P(('pod', 'data'))
- embed_table: bfloat16 [50304, 768], P('tensor')
- norm_gain: bfloat16 [768], replicated
- w_in: bfloat16 [768, 3072], P(None, 'tensor')
- w_out: bfloat16 [3072, 768], P('tensor')
- d_out: bfloat16 [32768, 768], P(('pod', 'data', 'tensor'))
Outputs:
- output 1: bfloat16 [32768, 768], P(('pod', 'data', 'tensor'))
- output 2: float32 [50304, 768], P(('pod', 'tensor'))
- output 3: float32 [768, 3072], P('pod', 'tensor')
- output 4: float32 [3072, 768], P(('pod', 'tensor'))
All inputs are finite; a program needn't handle non-finite values.
Results may differ from a plain program's by a relative error of at most 0.0057936.
Values are sent between devices in bfloat16 or wider.
A program may use at most 768 MiB of HBM per device.

v0:
```python
import jax
import jax.numpy as jnp
from jax import lax
from jax.sharding import PartitionSpec as P

NORM_EPS = 1e-6


def gelu_tanh(value):
    return jax.nn.gelu(value, approximate=True)


def solution(mesh):
    tok_spec = P(("pod", "data", "tensor"), None)

    def per_device(token_ids, embed_table, norm_gain, w_in, w_out, d_out):
        shard_rows = embed_table.shape[0]
        tp_rank = lax.axis_index("tensor")
        local_ids = token_ids - tp_rank * shard_rows
        is_owned = (local_ids >= 0) & (local_ids < shard_rows)
        picked = jnp.take(embed_table, jnp.where(is_owned, local_ids, 0), axis=0)
        partial_rows = jnp.where(is_owned[:, None], picked, jnp.zeros_like(picked))
        embedded = lax.psum_scatter(partial_rows, "tensor", scatter_dimension=0, tiled=True)
        gain_f32 = norm_gain.astype(jnp.float32)
        x_f32 = embedded.astype(jnp.float32)
        inv_rms = lax.rsqrt(jnp.mean(x_f32 * x_f32, axis=-1, keepdims=True) + NORM_EPS)
        x_hat = x_f32 * inv_rms
        normed = (x_hat * gain_f32).astype(jnp.bfloat16)
        normed_all = lax.all_gather(normed, "tensor", axis=0, tiled=True)
        pre_gelu = jnp.dot(normed_all, w_in, preferred_element_type=jnp.float32).astype(jnp.bfloat16)
        hidden_f32, gelu_pull = jax.vjp(gelu_tanh, pre_gelu.astype(jnp.float32))
        hidden = hidden_f32.astype(jnp.bfloat16)
        mlp_part = jnp.dot(hidden, w_out, preferred_element_type=jnp.float32)
        mlp_out = lax.psum_scatter(mlp_part, "tensor", scatter_dimension=0, tiled=True)
        block_out = (x_f32 + mlp_out).astype(jnp.bfloat16)

        grad_all = lax.all_gather(d_out, "tensor", axis=0, tiled=True)
        grad_hidden = lax.dot_general(grad_all, w_out, (((1,), (1,)), ((), ())), preferred_element_type=jnp.float32)
        grad_pre = gelu_pull(grad_hidden)[0].astype(jnp.bfloat16)
        grad_w_out = lax.dot_general(hidden, grad_all, (((0,), (0,)), ((), ())), preferred_element_type=jnp.float32)
        grad_w_in = lax.dot_general(normed_all, grad_pre, (((0,), (0,)), ((), ())), preferred_element_type=jnp.float32)
        norm_part = lax.dot_general(grad_pre, w_in, (((1,), (1,)), ((), ())), preferred_element_type=jnp.float32)
        d_normed = lax.psum_scatter(norm_part, "tensor", scatter_dimension=0, tiled=True)
        d_hat = d_normed * gain_f32
        d_norm_in = inv_rms * (d_hat - x_hat * jnp.mean(d_hat * x_hat, axis=-1, keepdims=True))
        d_embed = (d_out.astype(jnp.float32) + d_norm_in).astype(jnp.bfloat16)
        d_embed_all = lax.all_gather(d_embed, "tensor", axis=0, tiled=True)
        grad_table = jax.ops.segment_sum(d_embed_all.astype(jnp.float32), jnp.where(is_owned, local_ids, shard_rows), num_segments=shard_rows)
        grad_table = lax.psum(grad_table, "data")
        grad_w_in = lax.psum(grad_w_in, "data")
        grad_w_out = lax.psum(grad_w_out, "data")
        return block_out, grad_table, grad_w_in, grad_w_out

    return jax.shard_map(
        per_device,
        mesh=mesh,
        in_specs=(P(("pod", "data")), P("tensor", None), P(None), P(None, "tensor"), P("tensor", None), tok_spec),
        out_specs=(tok_spec, P(("pod", "tensor"), None), P("pod", "tensor"), P(("pod", "tensor"), None)),
        check_vma=False,
    )
```

profile of v0, /device:TPU:97, one launch (start us, length us, event | category | flops | bytes accessed | tf_op | source)
XLA Modules:
  0.0 1094.7 jit_solution(7529653243916610356)
XLA Ops:
  7.2 0.0 copy-start
  7.2 0.1 reduce-scatter.4.cloned.1.call-start
  7.3 0.8 compare_and_fusion.1
  8.1 1.4 subtract_select_fusion
  9.5 42.0 %gather_fusion = bf16[8192,768]{1,0:T(8,128)(2,1)} fusion(bf16[6288,768]{1,0:T(8,128)(2,1)} %param.7, s32[8192]{0:T(1024)S(1)} %get-tuple-element.10), kind=kCustom, calls=%fused_computation | custom fusion | bytes 25198592 | tf_op jit(solution)/shard_map/jit(_take)/gather | solution.py:21
  51.5 13.0 %select_select_fusion = bf16[8192,768]{1,0:T(8,128)(2,1)} fusion(bf16[8192,768]{1,0:T(8,128)(2,1)} %gather_fusion, pred[8192]{0:T(1024)(128)(4,1)S(1)} %get-tuple-element.12, pred[8192]{0:T(1024)(128)(4,1)S(1)} %get-tuple-element.11), kind=kLoop, calls=%fused_computation.19 | loop fusion | flops 12582912 | bytes 25182208 | tf_op jit(solution)/shard_map/jit(_where)/select_n | solution.py:22
  64.5 0.1 reduce-scatter.4.cloned.1.call-update
  64.6 0.1 all-gather.6.cloned.1.call-start
  64.7 0.7 all-gather.6.cloned.1.call-update
  65.4 0.1 all-gather.4.cloned.1.call-start
  65.5 0.0 copy-done.6
  65.5 72.6 %reduce-scatter.4.cloned.1.call-done = bf16[1024,768]{1,0:T(8,128)(2,1)} async-done(((bf16[8192,768]{1,0:T(8,128)(2,1)}), bf16[1024,768]{1,0:T(8,128)(2,1)}) %reduce-scatter.4.cloned.1.call-update) | async-done | bytes 1572880 | tf_op jit(solution)/shard_map/reduce_scatter | solution.py:23
  138.1 1.8 fusion.22
  139.9 3.0 fusion.16
  142.9 0.1 all-gather.4.cloned.1.call-update
  142.9 0.2 reduce-scatter.8.cloned.1.call-start
  143.2 61.9 %all-gather.6.cloned.1.call-done = bf16[8192,768]{1,0:T(8,128)(2,1)} async-done(((bf16[1024,768]{1,0:T(8,128)(2,1)}), bf16[8192,768]{1,0:T(8,128)(2,1)}) %all-gather.6.cloned.1.call-update) | async-done | bytes 12582928 | tf_op jit(solution)/shard_map/all_gather | solution.py:37
  205.0 0.0 copy-done.7
  205.0 12.4 %fusion.29 = f32[8192,384]{1,0:T(8,128)} fusion(bf16[8192,768]{1,0:T(8,128)(2,1)} %all-gather.6.cloned.1.call-done, bf16[384,768]{1,0:T(8,128)(2,1)S(1)} %copy-done.7), kind=kOutput, calls=%fused_computation.45 | convolution fusion | flops 4831838208 | bytes 25755648 | tf_op jit(solution)/shard_map/dot_general | solution.py:38
  217.5 54.9 %all-gather.4.cloned.1.call-done = bf16[8192,768]{1,0:T(8,128)(2,1)} async-done(((bf16[1024,768]{1,0:T(8,128)(2,1)}), bf16[8192,768]{1,0:T(8,128)(2,1)}) %all-gather.4.cloned.1.call-update) | async-done | bytes 12582928 | tf_op jit(solution)/shard_map/all_gather | solution.py:29
  272.4 0.0 copy-done
  272.4 21.1 %fusion.5 = (bf16[8192,384]{1,0:T(8,128)(2,1)S(1)}, bf16[8192,384]{1,0:T(8,128)(2,1)}) fusion(f32[8192,384]{1,0:T(8,128)} %fusion.29, bf16[8192,768]{1,0:T(8,128)(2,1)} %all-gather.4.cloned.1.call-done, bf16[768,384]{1,0:T(8,128)(2,1)S(1)} %copy-done), kind=kOutput, calls=%fused_computation.12 | convolution fusion | flops 4901044224 | bytes 38338560 | tf_op jit(solution)/shard_map/dot_general | solution.py:30
  293.5 2.7 copy-done.3
  296.2 11.7 %fusion.30 = f32[8192,768]{1,0:T(8,128)} fusion(bf16[8192,384]{1,0:T(8,128)(2,1)S(1)} %get-tuple-element.13, bf16[768,384]{1,0:T(8,128)(2,1)S(1)} %copy-done), kind=kOutput, calls=%fused_computation.46 | convolution fusion | flops 4831838208 | bytes 32047104 | tf_op jit(solution)/shard_map/dot_general | solution.py:42
  307.9 0.1 reduce-scatter.8.cloned.1.call-update
  308.0 0.3 reduce-scatter.6.cloned.1.call-start
  308.3 15.6 %fusion.27 = f32[8192,768]{1,0:T(8,128)} fusion(bf16[384,768]{1,0:T(8,128)(2,1)S(1)} %copy-done.7, bf16[8192,384]{1,0:T(8,128)(2,1)} %get-tuple-element.14), kind=kOutput, calls=%fused_computation.44 | convolution fusion | flops 4863295488 | bytes 32047104 | tf_op jit(solution)/shard_map/dot_general | solution.py:33
  323.9 0.1 reduce-scatter.6.cloned.1.call-update
  323.9 0.1 all-gather.8.cloned.1.call-start
  324.0 112.6 %reduce-scatter.8.cloned.1.call-done = f32[1024,768]{1,0:T(8,128)} async-done(((f32[8192,768]{1,0:T(8,128)}), f32[1024,768]{1,0:T(8,128)}) %reduce-scatter.8.cloned.1.call-update) | async-done | bytes 3145744 | tf_op jit(solution)/shard_map/reduce_scatter | solution.py:43
  436.5 0.0 copy-done.2
  436.6 2.7 fusion.17
  439.2 128.1 %reduce-scatter.6.cloned.1.call-done = f32[1024,768]{1,0:T(8,128)} async-done(((f32[8192,768]{1,0:T(8,128)}), f32[1024,768]{1,0:T(8,128)}) %reduce-scatter.6.cloned.1.call-update) | async-done | bytes 3145744 | tf_op jit(solution)/shard_map/reduce_scatter | solution.py:34
  567.3 5.1 fusion.21
  572.4 0.1 all-gather.8.cloned.1.call-update
  572.5 0.1 all-reduce.3.cloned.1.call-start
  572.5 12.3 %fusion.31 = f32[768,384]{1,0:T(8,128)} fusion(bf16[8192,768]{1,0:T(8,128)(2,1)} %all-gather.4.cloned.1.call-done, bf16[8192,384]{1,0:T(8,128)(2,1)} %copy-done.3), kind=kOutput, calls=%fused_computation.47 | convolution fusion | flops 4831838208 | bytes 20054016 | tf_op jit(solution)/shard_map/dot_general | solution.py:41
  584.8 13.2 %fusion.25 = f32[384,768]{1,0:T(8,128)} fusion(bf16[8192,768]{1,0:T(8,128)(2,1)} %all-gather.6.cloned.1.call-done, bf16[8192,384]{1,0:T(8,128)(2,1)} %get-tuple-element.14), kind=kOutput, calls=%fused_computation.43 | convolution fusion | flops 4863295488 | bytes 20054016 | tf_op jit(solution)/shard_map/dot_general | solution.py:40
  598.1 39.8 %all-gather.8.cloned.1.call-done = bf16[8192,768]{1,0:T(8,128)(2,1)} async-done(((bf16[1024,768]{1,0:T(8,128)(2,1)}), bf16[8192,768]{1,0:T(8,128)(2,1)}) %all-gather.8.cloned.1.call-update) | async-done | bytes 12582928 | tf_op jit(solution)/shard_map/all_gather | solution.py:47
  637.9 63.1 %scatter_custom_fusion = f32[6288,768]{1,0:T(8,128)} fusion(s32[8192]{0:T(1024)} %get-tuple-element.9, bf16[8192,768]{1,0:T(8,128)(2,1)} %all-gather.8.cloned.1.call-done, f32[]{:T(128)} %constant.21.clone.1), kind=kCustom, calls=%fused_computation.2 | custom fusion | flops 12582912 | bytes 31900160 | tf_op jit(solution)/shard_map/scatter-add | solution.py:48
  701.1 0.1 all-reduce.3.cloned.1.call-update
  701.1 369.2 %all-reduce.3.cloned.1.call-done = (f32[6288,768]{1,0:T(8,128)}, f32[768,384]{1,0:T(8,128)}, f32[384,768]{1,0:T(8,128)}) async-done(((f32[6288,768]{1,0:T(8,128)}, f32[768,384]{1,0:T(8,128)}, f32[384,768]{1,0:T(8,128)}), (f32[6288,768]{1,0:T(8,128)}, f32[768,384]{1,0:T(8,128)}, f32[384,768]{1,0:T(8,128)})) %all-reduce.3.cloned.1.call-update) | async-done | bytes 21676048 | tf_op jit(solution)/shard_map/psum | solution.py:49
  1070.3 15.5 %copy.13 = f32[6288,768]{1,0:T(8,128)} copy(f32[6288,768]{1,0:T(8,128)} %get-tuple-element.16) | data formatting | bytes 38633472
  1085.8 0.0 copy-done.5
  1085.8 1.0 copy.14
  1086.8 0.0 copy-done.4
  1086.8 1.0 copy.15
  1087.8 0.0 copy-done.1
  (10 shorter events, 0.0 us)
Async XLA Ops:
  7.2 265.2 %copy-start = (bf16[768,384]{1,0:T(8,128)(2,1)S(1)}, bf16[768,384]{1,0:T(8,128)(2,1)}, u32[]{:S(2)}) copy-start(bf16[768,384]{1,0:T(8,128)(2,1)} %param.9) | copy-start | bytes 1769476
  7.2 130.9 %reduce-scatter.4.cloned.1.call-start = ((), (), s32[]{:S(2)}) async-start(), calls=%async_computation.3 | async-start | bytes 14155776 | tf_op jit(solution)/shard_map/reduce_scatter | solution.py:23
  64.5 1.0 copy-start.6
  64.5 140.5 %copy-start.7 = (bf16[384,768]{1,0:T(8,128)(2,1)S(1)}, bf16[384,768]{1,0:T(8,128)(2,1)}, u32[]{:S(2)}) copy-start(bf16[384,768]{1,0:T(8,128)(2,1)} %param.10) | copy-start | bytes 1769476
  64.6 140.4 %all-gather.6.cloned.1.call-start = ((), (), s32[]{:S(2)}) async-start(), calls=%async_computation.6 | async-start | bytes 14155776 | tf_op jit(solution)/shard_map/all_gather | solution.py:37
  65.4 207.0 %all-gather.4.cloned.1.call-start = ((), (), s32[]{:S(2)}) async-start(), calls=%async_computation.4 | async-start | bytes 14155776 | tf_op jit(solution)/shard_map/all_gather | solution.py:29
  142.9 293.6 %reduce-scatter.8.cloned.1.call-start = ((), (), s32[]{:S(2)}) async-start(), calls=%async_computation.7 | async-start | bytes 28311552 | tf_op jit(solution)/shard_map/reduce_scatter | solution.py:43
  293.5 2.7 copy-start.3
  308.0 259.3 %reduce-scatter.6.cloned.1.call-start = ((), (), s32[]{:S(2)}) async-start(), calls=%async_computation.5 | async-start | bytes 28311552 | tf_op jit(solution)/shard_map/reduce_scatter | solution.py:34
  323.8 112.7 %copy-start.2 = (bf16[1024,768]{1,0:T(8,128)(2,1)S(1)}, bf16[1024,768]{1,0:T(8,128)(2,1)}, u32[]{:S(2)}) copy-start(bf16[1024,768]{1,0:T(8,128)(2,1)} %reduce-scatter.4.cloned.1.call-done) | copy-start | bytes 4718596
  323.9 314.0 %all-gather.8.cloned.1.call-start = ((), (), s32[]{:S(2)}) async-start(), calls=%async_computation.8 | async-start | bytes 14155776 | tf_op jit(solution)/shard_map/all_gather | solution.py:47
  572.5 497.9 %all-reduce.3.cloned.1.call-start = ((), (), s32[]{:S(2)}) async-start(), calls=%async_computation.9 | async-start | bytes 43352064 | tf_op jit(solution)/shard_map/psum | solution.py:49
  1070.3 17.5 %copy-start.1 = (bf16[768,384]{1,0:T(8,128)(2,1)S(1)}, bf16[768,384]{1,0:T(8,128)(2,1)}, u32[]{:S(2)}) copy-start(bf16[768,384]{1,0:T(8,128)(2,1)} %param.9) | copy-start | bytes 1769476
  1070.3 15.5 %copy-start.5 = (f32[768,384]{1,0:T(8,128)S(1)}, f32[768,384]{1,0:T(8,128)}, u32[]{:S(2)}) copy-start(f32[768,384]{1,0:T(8,128)} %get-tuple-element.17) | copy-start | bytes 3538948
  1070.3 16.5 %copy-start.4 = (f32[384,768]{1,0:T(8,128)S(1)}, f32[384,768]{1,0:T(8,128)}, u32[]{:S(2)}) copy-start(f32[384,768]{1,0:T(8,128)} %get-tuple-element.18) | copy-start | bytes 3538948
Sparse Core Ops, SparseCore 0:
  64.7 73.3 reduce-scatter.3
  139.7 65.2 all-gather.5
  207.2 65.1 all-gather.3
  308.1 128.3 reduce-scatter.7
  438.8 128.5 reduce-scatter.5
  572.6 65.2 all-gather.7
  701.2 369.0 all-reduce.2
where the time goes:
time: 1100 us; the launch traced here: 1090 us
  waiting for transfers between devices  840 us (76%)
  other arithmetic  90.9 us (8%)
  matrix products  86.4 us (8%)
  local copies, waits for them, and re-layouts  62.2 us (6%)
  between operations  14.2 us (1%)
    psum x1, waiting for transfers between devices, per_device(): grad_table = lax.psum(grad_table, 'data')  369 us
    reduce_scatter x1, waiting for transfers between devices, per_device(): lax.psum_scatter(mlp_part, 'tensor', scatter_dimension=0, tiled=True)  128 us
    reduce_scatter x1, waiting for transfers between devices, per_device(): lax.psum_scatter(norm_part, 'tensor', scatter_dimension=0, tiled=True)  113 us
    reduce_scatter x1, waiting for transfers between devices, per_device(): lax.psum_scatter(partial_rows, 'tensor', scatter_dimension=0, tiled=True)  72.6 us
    scatter-add x1, other arithmetic, per_device(): jax.ops.segment_sum(d_embed_all.astype(jnp.float32), jnp.where(is_owned,...  63.1 us
    all_gather x1, waiting for transfers between devices, per_device(): grad_all = lax.all_gather(d_out, 'tensor', axis=0, tiled=True)  61.9 us
    all_gather x1, waiting for transfers between devices, per_device(): normed_all = lax.all_gather(normed, 'tensor', axis=0, tiled=True)  54.9 us
    gather x1, local copies, waits for them, and re-layouts, per_device(): picked = jnp.take(embed_table, jnp.where(is_owned, local_ids, 0), axis=0)  42 us
  transfers between devices with their start and end apart: 7, of which 7 were waited for; matrix products, arithmetic and copies ran while one was open for 6% of the time, Pallas kernels for 0%

commit v1 on v0

v1 whole, which is shorter than its diff:
```python
import functools

import jax
import jax.numpy as jnp
from jax import lax
from jax.experimental import pallas as pl
from jax.experimental.pallas import tpu as pltpu
from jax.sharding import PartitionSpec as P

NORM_EPS = 1e-6
HALVES = 2
F32 = jnp.float32
BF16 = jnp.bfloat16
NT = (((1,), (1,)), ((), ()))
TN = (((0,), (0,)), ((), ()))


def gelu_tanh(value):
    return jax.nn.gelu(value, approximate=True)


def list_kernel(rows, bits, per_part, n_parts, base_ref, ids_ref, list_ref):
    base = base_ref[0]
    n_tok = per_part * n_parts

    def one_part(part, count):
        list_ref[n_tok + part] = count

        def one_token(pos, count):
            local = ids_ref[part * per_part + pos] - base
            list_ref[count] = (pos << bits) | (local & ((1 << bits) - 1))
            owned = jnp.logical_and(local >= 0, local < rows)
            return count + owned.astype(jnp.int32)

        return lax.fori_loop(0, per_part, one_token, count, unroll=16)

    list_ref[n_tok + n_parts] = lax.fori_loop(0, n_parts, one_part, jnp.int32(0))


def list_owned(token_ids, rows, rank, n_parts):
    n_tok = token_ids.shape[0]
    bits = rows.bit_length()
    size = n_tok + 128
    return pl.pallas_call(
        functools.partial(list_kernel, rows, bits, n_tok // n_parts, n_parts),
        out_shape=jax.ShapeDtypeStruct((size,), jnp.int32),
        in_specs=[pl.BlockSpec(memory_space=pltpu.SMEM)] * 2,
        out_specs=pl.BlockSpec(memory_space=pltpu.SMEM),
        cost_estimate=pl.CostEstimate(flops=n_tok * 4000, bytes_accessed=8 * n_tok, transcendentals=0),
    )((rank * rows)[None].astype(jnp.int32), token_ids)


def scatter_kernel(bits, n_dev, half, n_tok, size, list_ref, part_ref, *refs):
    out_ref, table, stage, sem = refs[-4:]
    step = pl.program_id(0)
    rows = table.shape[0]
    tile = 8

    @pl.when(step == 0)
    def _():
        if len(refs) > 4:
            copy = pltpu.make_async_copy(refs[0], table, sem)
            copy.start()
            copy.wait()
        else:

            def clear(i, carry):
                table[pl.ds(pl.multiple_of(i * tile, tile), tile), :] = jnp.zeros((tile, table.shape[1]), F32)
                return carry

            lax.fori_loop(0, rows // tile, clear, 0, unroll=2)

    stage[...] = part_ref[...].astype(F32)

    replica = step // n_dev
    dev = step - replica * n_dev
    base = replica * size
    first = list_ref[base + n_tok + dev * HALVES + half]
    last = list_ref[base + n_tok + dev * HALVES + half + 1]
    mask = (1 << bits) - 1

    def add(k):
        entry = list_ref[base + k]
        pos = entry >> bits
        row = entry & mask
        table[pl.ds(row, 1), :] = table[pl.ds(row, 1), :] + stage[pl.ds(pos, 1), :]

    n_quads = (last - first) >> 2

    def quad(i, carry):
        for j in range(4):
            add(first + i * 4 + j)
        return carry

    lax.fori_loop(0, n_quads, quad, 0)

    def single(k, carry):
        add(k)
        return carry

    lax.fori_loop(first + n_quads * 4, last, single, 0)

    @pl.when(step == pl.num_programs(0) - 1)
    def _():
        copy = pltpu.make_async_copy(table, out_ref, sem)
        copy.start()
        copy.wait()


def scatter_rows(lists, part, half, table, rows, n_dev, n_rep):
    size = lists.shape[0] // n_rep
    total, dim = part.shape
    per_part = total // (n_dev * n_rep)
    n_tok = per_part * HALVES * n_dev
    more = [] if table is None else [table]
    return pl.pallas_call(
        functools.partial(scatter_kernel, rows.bit_length(), n_dev, half, n_tok, size),
        out_shape=jax.ShapeDtypeStruct((rows, dim), F32),
        grid_spec=pltpu.PrefetchScalarGridSpec(
            num_scalar_prefetch=1,
            grid=(n_dev * n_rep,),
            in_specs=[pl.BlockSpec((per_part, dim), lambda i, *_: (i, 0))] + [pl.BlockSpec(memory_space=pl.ANY)] * len(more),
            out_specs=pl.BlockSpec(memory_space=pl.ANY),
            scratch_shapes=[
                pltpu.VMEM((rows, dim), F32),
                pltpu.VMEM((per_part, dim), F32),
                pltpu.SemaphoreType.DMA,
            ],
        ),
        input_output_aliases={2: 0} if more else {},
        compiler_params=pltpu.CompilerParams(vmem_limit_bytes=32 << 20, dimension_semantics=("arbitrary",)),
        cost_estimate=pl.CostEstimate(
            flops=total * 1000000, bytes_accessed=8 * rows * dim + 2 * total * dim, transcendentals=0
        ),
    )(lists, part, *more)


def solution(mesh):
    tok_spec = P(("pod", "data", "tensor"), None)
    n_dev = mesh.shape["tensor"]
    n_rep = mesh.shape["data"]

    def body(token_ids, embed_table, norm_gain, w_in, w_out, d_out):
        shard_rows, _ = embed_table.shape
        rank = lax.axis_index("tensor")
        replica = lax.axis_index("data")
        n_tok = token_ids.shape[0]
        per_dev = n_tok // n_dev
        half = per_dev // HALVES

        piece = w_out.shape[0] // n_rep
        both = ("tensor", "data")
        w2 = lax.all_gather(lax.dynamic_slice_in_dim(w_out, replica * piece, piece), both, axis=0, tiled=True)
        w1t = lax.all_gather(lax.dynamic_slice_in_dim(w_in.T, replica * piece, piece), both, axis=0, tiled=True)

        ids_by_dev = token_ids.reshape(n_dev, HALVES, half)
        gain_f32 = norm_gain.astype(F32)

        x_halves = []
        for k in range(HALVES):
            local_ids = ids_by_dev[:, k].reshape(-1) - rank * shard_rows
            is_owned = (local_ids >= 0) & (local_ids < shard_rows)
            picked = jnp.take(embed_table, jnp.where(is_owned, local_ids, 0), axis=0)
            partial_rows = jnp.where(is_owned[:, None], picked, jnp.zeros_like(picked))
            x_halves.append(lax.psum_scatter(partial_rows, "tensor", scatter_dimension=0, tiled=True))

        lists = list_owned(token_ids, shard_rows, rank, n_dev * HALVES)
        lists = lax.all_gather(lists, "data", axis=0, tiled=True)

        outs, grads, saved = [], [], []
        for k in range(HALVES):
            x_half = x_halves[k]
            if k > 0:
                x_half, _ = lax.optimization_barrier((x_half, d_embed))
            x_f32 = x_half.astype(F32)
            d_half = lax.slice_in_dim(d_out, k * half, (k + 1) * half)
            inv_rms = lax.rsqrt(jnp.mean(x_f32 * x_f32, axis=-1, keepdims=True) + NORM_EPS)
            x_hat = x_f32 * inv_rms
            normed = (x_hat * gain_f32).astype(BF16)
            pre_gelu = lax.dot_general(normed, w1t, NT, preferred_element_type=F32).astype(BF16)
            hidden_f32, gelu_pull = jax.vjp(gelu_tanh, pre_gelu.astype(F32))
            hidden = hidden_f32.astype(BF16)
            grad_hidden = lax.dot_general(d_half, w2, NT, preferred_element_type=F32)
            grad_pre = gelu_pull(grad_hidden)[0].astype(BF16)
            d_normed = jnp.dot(grad_pre, w1t, preferred_element_type=F32)
            d_hat = d_normed * gain_f32
            d_norm_in = inv_rms * (d_hat - x_hat * jnp.mean(d_hat * x_hat, axis=-1, keepdims=True))
            d_embed = (d_half.astype(F32) + d_norm_in).astype(BF16)
            grads.append(lax.all_gather(d_embed, ("data", "tensor"), axis=0, tiled=True))
            normed, hidden, grad_pre, d_half, _ = lax.optimization_barrier((normed, hidden, grad_pre, d_half, d_embed))
            saved.append((normed, hidden, grad_pre, d_half))
            mlp_out = jnp.dot(hidden, w2, preferred_element_type=F32)
            outs.append((x_f32 + mlp_out).astype(BF16))
        block_out = jnp.concatenate(outs, axis=0)

        grad_w2 = sum(lax.dot_general(h, d, TN, preferred_element_type=F32) for _, h, _, d in saved)
        grad_w1t = sum(lax.dot_general(u, n, TN, preferred_element_type=F32) for n, _, u, _ in saved)
        grad_w2 = lax.psum_scatter(grad_w2, both, scatter_dimension=0, tiled=True)
        grad_w1t = lax.psum_scatter(grad_w1t, both, scatter_dimension=0, tiled=True)
        grad_w2 = lax.all_gather(grad_w2, "data", axis=0, tiled=True)
        grad_w1t = lax.all_gather(grad_w1t, "data", axis=0, tiled=True)

        grad_table = None
        for k in range(HALVES):
            grad_table = scatter_rows(lists, grads[k], k, grad_table, shard_rows, n_dev, n_rep)
        return block_out, grad_table, grad_w1t.T, grad_w2

    return jax.shard_map(
        body,
        mesh=mesh,
        in_specs=(P(("pod", "data")), P("tensor", None), P(None), P(None, "tensor"), P("tensor", None), tok_spec),
        out_specs=(tok_spec, P(("pod", "tensor"), None), P("pod", "tensor"), P(("pod", "tensor"), None)),
        check_vma=False,
    )
```

time: 1100 us -> 634 us (0.58)
  waiting for transfers between devices: 840 us -> 314 us
  Pallas kernels: 0 us -> 137 us
  other arithmetic: 90.9 us -> 26.1 us
  matrix products: 86.4 us -> 68.4 us
  blocking collectives: 0 us -> 11.3 us
    psum x1 -> x0, waiting for transfers between devices: 369 us -> none  [per_device(): grad_table = lax.psum(grad_table, 'data')]
    pallas_call x0 -> x3, Pallas kernels: none -> 137 us  [the longest x2 101 us: scatter_rows(): pl.pallas_call(functools.partial(scatter_kernel, rows.bit_length(), n_dev...]
    reduce_scatter x3 -> x4, waiting for transfers between devices: 313 us -> 178 us  [the longest x1 90.5 us: body(): grad_w2 = lax.psum_scatter(grad_w2, both, scatter_dimension=0, tiled=True)]
    scatter-add x1 -> x0, other arithmetic: 63.1 us -> none  [per_device(): jax.ops.segment_sum(d_embed_all.astype(jnp.float32), jnp.where(is_owned,...]
    all_gather x3 -> x6, waiting for transfers between devices: 157 us -> 134 us  [the longest x2 86.6 us: body(): lax.all_gather(d_embed, ('data', 'tensor'), axis=0, tiled=True)]
    dot_general x6 -> x12, matrix products: 86.4 us -> 68.4 us  [the longest x2 15 us: body(): grad_hidden = lax.dot_general(d_half, w2, NT, preferred_element_type=F32)]
    unnamed x19 -> x45, local copies, waits for them, and re-layouts: 20.2 us -> 6.55 us
    all_gather x0 -> x1, blocking collectives: none -> 11.3 us  [body(): lists = lax.all_gather(lists, 'data', axis=0, tiled=True)]
  transfers between devices with their start and end apart: 7 -> 10, of which waited for: 7 -> 7; matrix products, arithmetic and copies ran while one was open for 6% -> 14% of each run, Pallas kernels for 0% -> 14%
where the time goes in v1:
time: 634 us; the launch traced here: 632 us
  waiting for transfers between devices  314 us (50%)
  Pallas kernels  137 us (22%)
  matrix products  68.4 us (11%)
  local copies, waits for them, and re-layouts  58.4 us (9%)
  other arithmetic  26.1 us (4%)
  between operations  16.2 us (3%)
  blocking collectives  11.3 us (2%)
    pallas_call x2, Pallas kernels, scatter_rows(): pl.pallas_call(functools.partial(scatter_kernel, rows.bit_length(), n_dev...  101 us
    reduce_scatter x1, waiting for transfers between devices, body(): grad_w2 = lax.psum_scatter(grad_w2, both, scatter_dimension=0, tiled=True)  90.5 us
    all_gather x2, waiting for transfers between devices, body(): lax.all_gather(d_embed, ('data', 'tensor'), axis=0, tiled=True)  86.6 us
    reduce_scatter x1, waiting for transfers between devices, body(): grad_w1t = lax.psum_scatter(grad_w1t, both, scatter_dimension=0, tiled=True)  74.6 us
    gather x2, local copies, waits for them, and re-layouts, body(): picked = jnp.take(embed_table, jnp.where(is_owned, local_ids, 0), axis=0)  48.1 us
    all_gather x1, waiting for transfers between devices, body(): lax.all_gather(lax.dynamic_slice_in_dim(w_out, replica * piece, piece), b...  42.9 us
    pallas_call x1, Pallas kernels, list_owned(): pl.pallas_call(functools.partial(list_kernel, rows, bits, n_tok // n_part...  36.6 us
    select_n x2, other arithmetic, body(): partial_rows = jnp.where(is_owned[:, None], picked, jnp.zeros_like(picked))  16 us
  transfers between devices with their start and end apart: 10, of which 7 were waited for; matrix products, arithmetic and copies ran while one was open for 14% of the time, Pallas kernels for 14%

profile of v1, /device:TPU:97, one launch (start us, length us, event | category | flops | bytes accessed | tf_op | source)
XLA Modules:
  0.0 632.0 jit_solution(10302001624569081852)
XLA Ops:
  8.1 0.8 reshape.61
  9.0 24.0 %gather_fusion = bf16[4096,768]{1,0:T(8,128)(2,1)} fusion(bf16[6288,768]{1,0:T(8,128)(2,1)} %param.9, s32[4096]{0:T(1024)S(1)} %fusion.44), kind=kCustom, calls=%fused_computation.clone | custom fusion | bytes 12599296 | tf_op jit(solution)/shard_map/jit(_take)/gather | solution.py:163
  33.1 8.0 %select_select_fusion.1 = bf16[4096,768]{1,0:T(8,128)(2,1)} fusion(bf16[4096,768]{1,0:T(8,128)(2,1)} %gather_fusion, pred[4096]{0:T(1024)(128)(4,1)S(1)} %get-tuple-element.36, pred[4096]{0:T(1024)(128)(4,1)S(1)} %get-tuple-element.35), kind=kLoop, calls=%fused_computation.37 | loop fusion | flops 6291456 | bytes 12591104 | tf_op jit(solution)/shard_map/jit(_where)/select_n | solution.py:164
  41.2 0.1 constant_dynamic-slice_fusion.1
  41.4 0.8 copy.20
  42.3 1.6 constant_dynamic-slice_fusion
  44.0 24.0 %gather_fusion.1 = bf16[4096,768]{1,0:T(8,128)(2,1)} fusion(bf16[6288,768]{1,0:T(8,128)(2,1)} %param.9, s32[4096]{0:T(1024)S(1)} %fusion.45), kind=kCustom, calls=%fused_computation.1.clone | custom fusion | bytes 12599296 | tf_op jit(solution)/shard_map/jit(_take)/gather | solution.py:163
  68.1 8.0 %select_select_fusion = bf16[4096,768]{1,0:T(8,128)(2,1)} fusion(bf16[4096,768]{1,0:T(8,128)(2,1)} %gather_fusion.1, pred[4096]{0:T(1024)(128)(4,1)S(1)} %get-tuple-element.38, pred[4096]{0:T(1024)(128)(4,1)S(1)} %get-tuple-element.37), kind=kLoop, calls=%fused_computation.36 | loop fusion | flops 6291456 | bytes 12591104 | tf_op jit(solution)/shard_map/jit(_where)/select_n | solution.py:164
  76.2 0.2 reduce-scatter.9.cloned.1.call-start
  76.4 0.4 copy-done.13
  76.8 0.8 copy-done.8
  77.6 1.3 fusion.48
  78.8 12.9 %reduce-scatter.5.cloned.1.call-done = bf16[512,768]{1,0:T(8,128)(2,1)} async-done(((bf16[4096,768]{1,0:T(8,128)(2,1)}), bf16[512,768]{1,0:T(8,128)(2,1)}) %reduce-scatter.5.cloned.1.call-update) | async-done | bytes 786448 | tf_op jit(solution)/shard_map/reduce_scatter | solution.py:165
  91.7 1.4 fusion.40
  93.2 1.4 fusion.34
  94.6 4.6 all-gather.8.cloned.1.call-done
  99.2 7.6 %fusion.11 = (bf16[512,3072]{1,0:T(8,128)(2,1)}, bf16[512,3072]{1,0:T(8,128)(2,1)}) fusion(bf16[512,768]{1,0:T(8,128)(2,1)S(1)} %fusion.34, bf16[3072,768]{1,0:T(8,128)(2,1)} %all-gather.8.cloned.1.call-done), kind=kOutput, calls=%fused_computation.23 | convolution fusion | flops 2433220608 | bytes 11796480 | tf_op jit(solution)/shard_map/dot_general | solution.py:180
  106.8 42.9 %all-gather.10.cloned.1.call-done = bf16[3072,768]{1,0:T(8,128)(2,1)} async-done(((bf16[96,768]{1,0:T(8,128)(2,1)}), bf16[3072,768]{1,0:T(8,128)(2,1)}) %all-gather.10.cloned.1.call-update) | async-done | bytes 4718608 | tf_op jit(solution)/shard_map/all_gather | solution.py:153
  149.6 8.6 %fusion.7 = bf16[512,3072]{1,0:T(8,128)(2,1)S(1)} fusion(bf16[512,3072]{1,0:T(8,128)(2,1)} %get-tuple-element.46, bf16[3072,768]{1,0:T(8,128)(2,1)} %all-gather.10.cloned.1.call-done, bf16[1024,768]{1,0:T(8,128)(2,1)S(1)} %copy-done.8), kind=kOutput, calls=%fused_computation.19 | convolution fusion | flops 2448949248 | bytes 11796480 | tf_op jit(solution)/shard_map/dot_general | solution.py:183
  158.2 2.7 fusion.35
  161.0 1.4 fusion.39
  162.3 1.4 fusion.42
  163.7 1.5 fusion.28
  165.3 7.3 %fusion.17 = (bf16[512,3072]{1,0:T(8,128)(2,1)}, bf16[512,3072]{1,0:T(8,128)(2,1)S(1)}) fusion(bf16[512,768]{1,0:T(8,128)(2,1)S(1)} %fusion.28, bf16[3072,768]{1,0:T(8,128)(2,1)} %all-gather.8.cloned.1.call-done), kind=kOutput, calls=%fused_computation.29 | convolution fusion | flops 2433220608 | bytes 11796480 | tf_op jit(solution)/shard_map/dot_general | solution.py:180
  172.6 6.5 %fusion.4 = bf16[512,3072]{1,0:T(8,128)(2,1)S(1)} fusion(bf16[512,3072]{1,0:T(8,128)(2,1)S(1)} %get-tuple-element.42, bf16[3072,768]{1,0:T(8,128)(2,1)S(1)} %bitcast.52, bf16[1024,768]{1,0:T(8,128)(2,1)S(1)} %copy-done.9), kind=kOutput, calls=%fused_computation.16 | convolution fusion | flops 2448949248 | bytes 11796480 | tf_op jit(solution)/shard_map/dot_general | solution.py:183
  179.1 2.7 fusion.29
  181.9 1.3 fusion.33
  183.2 5.0 fusion.49
  188.2 5.4 convolution_add_fusion.1
  193.7 5.0 fusion.50
  198.7 5.4 convolution_add_fusion
  204.2 74.6 %reduce-scatter.9.cloned.1.call-done = f32[96,768]{1,0:T(8,128)} async-done(((f32[3072,768]{1,0:T(8,128)}), f32[96,768]{1,0:T(8,128)}) %reduce-scatter.9.cloned.1.call-update) | async-done | bytes 294928 | tf_op jit(solution)/shard_map/reduce_scatter | solution.py:199
  279.0 90.5 %reduce-scatter.11.cloned.1.call-done = f32[96,768]{1,0:T(8,128)} async-done(((f32[3072,768]{1,0:T(8,128)}), f32[96,768]{1,0:T(8,128)}) %reduce-scatter.11.cloned.1.call-update) | async-done | bytes 294928 | tf_op jit(solution)/shard_map/reduce_scatter | solution.py:198
  369.6 0.6 all-gather.14.cloned.1.call-update
  370.3 0.6 all-gather.12.cloned.1.call-update
  370.8 36.6 %shard_map.93 = s32[8320]{0:T(1024)} custom-call(s32[1]{0:T(128)} %bitcast.5.base_ref, s32[8192]{0:T(1024)} %ids_ref.1), custom_call_target="tpu_custom_call" | custom-call | flops 32768000 | bytes 65536 | tf_op jit(solution)/shard_map/pallas_call | solution.py:44
  407.4 0.8 reshape.80
  408.2 11.3 %all-gather = s32[4,1,8320]{2,1,0:T(1,128)S(1)} all-gather(s32[1,1,8320]{2,1,0:T(1,128)S(1)} %reshape.80), channel_id=1, replica_groups=mesh['pod'=1,'data'=4,'tensor'=8] {'data'}, dimensions={0}, use_global_device_ids=true | all-gather | bytes 166400 | tf_op jit(solution)/shard_map/all_gather | solution.py:168
  419.5 0.3 reduce
  419.9 6.0 fusion.41
  426.0 6.4 %fusion.43 = bf16[512,768]{1,0:T(8,128)(2,1)S(1)} fusion(bf16[512,768]{1,0:T(8,128)(2,1)S(1)} %copy-done.3, bf16[512,3072]{1,0:T(8,128)(2,1)S(1)} %copy-done.5, bf16[3072,768]{1,0:T(8,128)(2,1)} %all-gather.10.cloned.1.call-done), kind=kOutput, calls=%fused_computation.69 | convolution fusion | flops 2417098752 | bytes 9437184 | tf_op jit(solution)/shard_map/dot_general | solution.py:192
  432.3 1.2 pad_maximum_fusion
  433.6 2.7 copy.17
  436.3 46.8 %all-gather.14.cloned.1.call-done.part_ref = bf16[16384,768]{1,0:T(8,128)(2,1)} async-done(((bf16[512,768]{1,0:T(8,128)(2,1)}), bf16[16384,768]{1,0:T(8,128)(2,1)}) %all-gather.14.cloned.1.call-update) | async-done | bytes 25165840 | tf_op jit(solution)/shard_map/all_gather | solution.py:189
  483.1 48.9 %shard_map.94.refs_0_ = f32[6288,768]{1,0:T(8,128)} custom-call(s32[33280]{0:T(1024)S(1)} %reshape.81.list_ref, bf16[16384,768]{1,0:T(8,128)(2,1)} %all-gather.14.cloned.1.call-done.part_ref), custom_call_target="tpu_custom_call" | custom-call | flops 16384000000 | bytes 63799296 | tf_op jit(solution)/shard_map/pallas_call | solution.py:116
  532.0 39.7 %all-gather.12.cloned.1.call-done.part_ref = bf16[16384,768]{1,0:T(8,128)(2,1)} async-done(((bf16[512,768]{1,0:T(8,128)(2,1)}), bf16[16384,768]{1,0:T(8,128)(2,1)}) %all-gather.12.cloned.1.call-update) | async-done | bytes 25165840 | tf_op jit(solution)/shard_map/all_gather | solution.py:189
  571.8 51.6 %shard_map.95 = f32[6288,768]{1,0:T(8,128)} custom-call(s32[33280]{0:T(1024)S(1)} %reshape.81.list_ref, bf16[16384,768]{1,0:T(8,128)(2,1)} %all-gather.12.cloned.1.call-done.part_ref, f32[6288,768]{1,0:T(8,128)} %shard_map.94.refs_0_), custom_call_target="tpu_custom_call", output_to_operand_aliasing={{}: (2, {})} | custom-call | flops 16384000000 | bytes 63799296 | tf_op jit(solution)/shard_map/pallas_call | solution.py:116
  623.4 1.0 copy.23
  (71 shorter events, 1.3 us)
Async XLA Ops:
  8.0 33.2 %copy-start = (bf16[768,384]{1,0:T(8,128)(2,1)S(1)}, bf16[768,384]{1,0:T(8,128)(2,1)}, u32[]{:S(2)}) copy-start(bf16[768,384]{1,0:T(8,128)(2,1)} %param.11) | copy-start | bytes 1769476
  8.1 83.7 %reduce-scatter.5.cloned.1.call-start = ((), (), s32[]{:S(2)}) async-start(), calls=%async_computation.4 | async-start | bytes 7077888 | tf_op jit(solution)/shard_map/reduce_scatter | solution.py:165
  41.1 58.0 %all-gather.8.cloned.1.call-start = ((), (), s32[]{:S(2)}) async-start(), calls=%async_computation.5 | async-start | bytes 4866048 | tf_op jit(solution)/shard_map/all_gather | solution.py:154
  42.2 107.4 %all-gather.10.cloned.1.call-start = ((), (), s32[]{:S(2)}) async-start(), calls=%async_computation.6 | async-start | bytes 4866048 | tf_op jit(solution)/shard_map/all_gather | solution.py:153
  44.0 118.4 %reduce-scatter.7.cloned.1.call-start = ((), (), s32[]{:S(2)}) async-start(), calls=%async_computation.7 | async-start | bytes 7077888 | tf_op jit(solution)/shard_map/reduce_scatter | solution.py:165
  76.1 0.7 copy-start.13
  76.1 1.5 copy-start.8
  76.2 202.6 %reduce-scatter.9.cloned.1.call-start = ((), (), s32[]{:S(2)}) async-start(), calls=%async_computation.10 | async-start | bytes 9732096 | tf_op jit(solution)/shard_map/reduce_scatter | solution.py:199
  94.6 12.2 %copy-start.12 = (bf16[512,768]{1,0:T(8,128)(2,1)}, bf16[512,768]{1,0:T(8,128)(2,1)S(1)}, u32[]{:S(2)}) copy-start(bf16[512,768]{1,0:T(8,128)(2,1)S(1)} %fusion.34) | copy-start | bytes 2359300
  149.6 8.6 %copy-start.2 = (bf16[512,768]{1,0:T(8,128)(2,1)S(1)}, bf16[512,768]{1,0:T(8,128)(2,1)}, u32[]{:S(2)}) copy-start(bf16[512,768]{1,0:T(8,128)(2,1)} %reduce-scatter.5.cloned.1.call-done) | copy-start | bytes 2359300
  149.6 8.6 %copy-start.14 = (bf16[3072,768]{1,0:T(8,128)(2,1)S(1)}, bf16[3072,768]{1,0:T(8,128)(2,1)}, u32[]{:S(2)}) copy-start(bf16[3072,768]{1,0:T(8,128)(2,1)} %all-gather.8.cloned.1.call-done) | copy-start | bytes 14155780
  158.2 2.7 copy-start.15
  163.7 8.9 %slice-start = ((s8[4718592]{0:T(1024)(128)(4,1)}), s8[4194304]{0:T(1024)(128)(4,1)S(1)}, s32[]{:S(2)}) async-start(s8[4718592]{0:T(1024)(128)(4,1)} %bitcast.51), calls=%async_computation.14 | async-start | bytes 8388608
  165.2 7.3 %copy-start.9 = (bf16[1024,768]{1,0:T(8,128)(2,1)S(1)}, bf16[1024,768]{1,0:T(8,128)(2,1)}, u32[]{:S(2)}) copy-start(bf16[1024,768]{1,0:T(8,128)(2,1)} %param.13) | copy-start | bytes 4718596
  165.2 7.3 %slice-start.1 = ((s8[4718592]{0:T(1024)(128)(4,1)}), s8[524288]{0:T(1024)(128)(4,1)S(1)}, s32[]{:S(2)}) async-start(s8[4718592]{0:T(1024)(128)(4,1)} %bitcast.51), calls=%async_computation.15 | async-start | bytes 1048576
  165.3 13.8 %slice-start.2 = ((s8[4718592]{0:T(1024)(128)(4,1)}), s8[4194304]{0:T(1024)(128)(4,1)S(1)}, s32[]{:S(2)}) async-start(s8[4718592]{0:T(1024)(128)(4,1)} %bitcast.53), calls=%async_computation.16 | async-start | bytes 8388608
  172.6 6.5 %copy-start.3 = (bf16[512,768]{1,0:T(8,128)(2,1)S(1)}, bf16[512,768]{1,0:T(8,128)(2,1)}, u32[]{:S(2)}) copy-start(bf16[512,768]{1,0:T(8,128)(2,1)} %reduce-scatter.7.cloned.1.call-done) | copy-start | bytes 2359300
  172.6 6.5 %slice-start.3 = ((s8[4718592]{0:T(1024)(128)(4,1)}), s8[524288]{0:T(1024)(128)(4,1)S(1)}, s32[]{:S(2)}) async-start(s8[4718592]{0:T(1024)(128)(4,1)} %bitcast.53), calls=%async_computation.17 | async-start | bytes 1048576
  179.1 2.7 copy-start.6
  183.2 5.0 copy-start.7
  193.6 5.1 copy-start.10
  193.6 175.9 %reduce-scatter.11.cloned.1.call-start = ((), (), s32[]{:S(2)}) async-start(), calls=%async_computation.12 | async-start | bytes 9732096 | tf_op jit(solution)/shard_map/reduce_scatter | solution.py:198
  193.7 5.0 copy-start.4
  204.1 229.5 %all-gather.16.cloned.1.call-start = ((), (), s32[]{:S(2)}) async-start(), calls=%async_computation.11 | async-start | bytes 1474560 | tf_op jit(solution)/shard_map/all_gather | solution.py:201
  278.9 157.4 %all-gather.18.cloned.1.call-start = ((), (), s32[]{:S(2)}) async-start(), calls=%async_computation.13 | async-start | bytes 1474560 | tf_op jit(solution)/shard_map/all_gather | solution.py:200
  369.5 113.6 %all-gather.14.cloned.1.call-start = ((), (), s32[]{:S(2)}) async-start(), calls=%async_computation.9 | async-start | bytes 25952256 | tf_op jit(solution)/shard_map/all_gather | solution.py:189
  370.2 201.6 %all-gather.12.cloned.1.call-start = ((), (), s32[]{:S(2)}) async-start(), calls=%async_computation.8 | async-start | bytes 25952256 | tf_op jit(solution)/shard_map/all_gather | solution.py:189
  419.9 6.0 copy-start.5
  532.0 91.3 %copy-start.11 = (f32[384,768]{1,0:T(8,128)S(1)}, f32[384,768]{1,0:T(8,128)}, u32[]{:S(2)}) copy-start(f32[384,768]{1,0:T(8,128)} %all-gather.18.cloned.1.call-done) | copy-start | bytes 3538948
  571.8 52.6 %copy-start.1 = (bf16[768,384]{1,0:T(8,128)(2,1)S(1)}, bf16[768,384]{1,0:T(8,128)(2,1)}, u32[]{:S(2)}) copy-start(bf16[768,384]{1,0:T(8,128)(2,1)} %param.11) | copy-start | bytes 1769476
Sparse Core Ops, SparseCore 0:
  41.2 50.4 reduce-scatter.4
  94.6 47.8 reduce-scatter.6
  279.0 20.8 all-gather.15
  369.7 20.8 all-gather.17
  392.4 90.6 all-gather.13
  485.6 86.1 all-gather.11
Sparse Core Ops, SparseCore 1:
  44.3 54.8 all-gather.7
  101.2 48.4 all-gather.9
  193.7 85.1 reduce-scatter.8
  282.4 87.0 reduce-scatter.10

commit v2 on v1

--- a/solution.py
+++ b/solution.py
@@ -4,6 +4,7 @@
 import jax.numpy as jnp
 from jax import lax
 from jax.experimental import pallas as pl
+from jax.experimental.layout import Layout, with_layout_constraint
 from jax.experimental.pallas import tpu as pltpu
 from jax.sharding import PartitionSpec as P
 
@@ -50,33 +51,26 @@
     )((rank * rows)[None].astype(jnp.int32), token_ids)
 
 
-def scatter_kernel(bits, n_dev, half, n_tok, size, list_ref, part_ref, *refs):
-    out_ref, table, stage, sem = refs[-4:]
+def scatter_kernel(bits, n_dev, n_tok, size, list_ref, part_ref, out_ref, table, stage, sem):
     step = pl.program_id(0)
     rows = table.shape[0]
     tile = 8
 
     @pl.when(step == 0)
     def _():
-        if len(refs) > 4:
-            copy = pltpu.make_async_copy(refs[0], table, sem)
-            copy.start()
-            copy.wait()
-        else:
-
-            def clear(i, carry):
-                table[pl.ds(pl.multiple_of(i * tile, tile), tile), :] = jnp.zeros((tile, table.shape[1]), F32)
-                return carry
-
-            lax.fori_loop(0, rows // tile, clear, 0, unroll=2)
+        def clear(i, carry):
+            table[pl.ds(pl.multiple_of(i * tile, tile), tile), :] = jnp.zeros((tile, table.shape[1]), F32)
+            return carry
+
+        lax.fori_loop(0, rows // tile, clear, 0, unroll=2)
 
     stage[...] = part_ref[...].astype(F32)
 
     replica = step // n_dev
     dev = step - replica * n_dev
     base = replica * size
-    first = list_ref[base + n_tok + dev * HALVES + half]
-    last = list_ref[base + n_tok + dev * HALVES + half + 1]
+    first = list_ref[base + n_tok + dev]
+    last = list_ref[base + n_tok + dev + 1]
     mask = (1 << bits) - 1
 
     def add(k):
@@ -107,19 +101,18 @@
         copy.wait()
 
 
-def scatter_rows(lists, part, half, table, rows, n_dev, n_rep):
+def scatter_rows(lists, part, rows, n_dev, n_rep):
     size = lists.shape[0] // n_rep
     total, dim = part.shape
     per_part = total // (n_dev * n_rep)
-    n_tok = per_part * HALVES * n_dev
-    more = [] if table is None else [table]
+    n_tok = per_part * n_dev
     return pl.pallas_call(
-        functools.partial(scatter_kernel, rows.bit_length(), n_dev, half, n_tok, size),
+        functools.partial(scatter_kernel, rows.bit_length(), n_dev, n_tok, size),
         out_shape=jax.ShapeDtypeStruct((rows, dim), F32),
         grid_spec=pltpu.PrefetchScalarGridSpec(
             num_scalar_prefetch=1,
             grid=(n_dev * n_rep,),
-            in_specs=[pl.BlockSpec((per_part, dim), lambda i, *_: (i, 0))] + [pl.BlockSpec(memory_space=pl.ANY)] * len(more),
+            in_specs=[pl.BlockSpec((per_part, dim), lambda i, *_: (i, 0))],
             out_specs=pl.BlockSpec(memory_space=pl.ANY),
             scratch_shapes=[
                 pltpu.VMEM((rows, dim), F32),
@@ -127,12 +120,11 @@
                 pltpu.SemaphoreType.DMA,
             ],
         ),
-        input_output_aliases={2: 0} if more else {},
         compiler_params=pltpu.CompilerParams(vmem_limit_bytes=32 << 20, dimension_semantics=("arbitrary",)),
         cost_estimate=pl.CostEstimate(
-            flops=total * 1000000, bytes_accessed=8 * rows * dim + 2 * total * dim, transcendentals=0
+            flops=total * 1000000, bytes_accessed=4 * rows * dim + 2 * total * dim, transcendentals=0
         ),
-    )(lists, part, *more)
+    )(lists, part)
 
 
 def solution(mesh):
@@ -143,15 +135,13 @@
     def body(token_ids, embed_table, norm_gain, w_in, w_out, d_out):
         shard_rows, _ = embed_table.shape
         rank = lax.axis_index("tensor")
-        replica = lax.axis_index("data")
         n_tok = token_ids.shape[0]
         per_dev = n_tok // n_dev
         half = per_dev // HALVES
 
-        piece = w_out.shape[0] // n_rep
-        both = ("tensor", "data")
-        w2 = lax.all_gather(lax.dynamic_slice_in_dim(w_out, replica * piece, piece), both, axis=0, tiled=True)
-        w1t = lax.all_gather(lax.dynamic_slice_in_dim(w_in.T, replica * piece, piece), both, axis=0, tiled=True)
+        w1t = with_layout_constraint(w_in.T, Layout(major_to_minor=(0, 1)))
+        w1t = lax.all_gather(w1t, "tensor", axis=0, tiled=True)
+        w2 = lax.all_gather(w_out, "tensor", axis=0, tiled=True)
 
         ids_by_dev = token_ids.reshape(n_dev, HALVES, half)
         gain_f32 = norm_gain.astype(F32)
@@ -164,7 +154,7 @@
             partial_rows = jnp.where(is_owned[:, None], picked, jnp.zeros_like(picked))
             x_halves.append(lax.psum_scatter(partial_rows, "tensor", scatter_dimension=0, tiled=True))
 
-        lists = list_owned(token_ids, shard_rows, rank, n_dev * HALVES)
+        lists = list_owned(token_ids, shard_rows, rank, n_dev)
         lists = lax.all_gather(lists, "data", axis=0, tiled=True)
 
         outs, grads, saved = [], [], []
@@ -186,23 +176,20 @@
             d_hat = d_normed * gain_f32
             d_norm_in = inv_rms * (d_hat - x_hat * jnp.mean(d_hat * x_hat, axis=-1, keepdims=True))
             d_embed = (d_half.astype(F32) + d_norm_in).astype(BF16)
-            grads.append(lax.all_gather(d_embed, ("data", "tensor"), axis=0, tiled=True))
+            grads.append(d_embed)
             normed, hidden, grad_pre, d_half, _ = lax.optimization_barrier((normed, hidden, grad_pre, d_half, d_embed))
             saved.append((normed, hidden, grad_pre, d_half))
             mlp_out = jnp.dot(hidden, w2, preferred_element_type=F32)
             outs.append((x_f32 + mlp_out).astype(BF16))
         block_out = jnp.concatenate(outs, axis=0)
+        grad_all = lax.all_gather(jnp.concatenate(grads, axis=0), ("data", "tensor"), axis=0, tiled=True)
 
         grad_w2 = sum(lax.dot_general(h, d, TN, preferred_element_type=F32) for _, h, _, d in saved)
         grad_w1t = sum(lax.dot_general(u, n, TN, preferred_element_type=F32) for n, _, u, _ in saved)
-        grad_w2 = lax.psum_scatter(grad_w2, both, scatter_dimension=0, tiled=True)
-        grad_w1t = lax.psum_scatter(grad_w1t, both, scatter_dimension=0, tiled=True)
-        grad_w2 = lax.all_gather(grad_w2, "data", axis=0, tiled=True)
-        grad_w1t = lax.all_gather(grad_w1t, "data", axis=0, tiled=True)
-
-        grad_table = None
-        for k in range(HALVES):
-            grad_table = scatter_rows(lists, grads[k], k, grad_table, shard_rows, n_dev, n_rep)
+        grad_w2 = lax.psum_scatter(grad_w2, "tensor", scatter_dimension=0, tiled=True)
+        grad_w1t = lax.psum_scatter(grad_w1t, "tensor", scatter_dimension=0, tiled=True)
+        grad_w2, grad_w1t = lax.psum((grad_w2, grad_w1t), "data")
+        grad_table = scatter_rows(lists, grad_all, shard_rows, n_dev, n_rep)
         return block_out, grad_table, grad_w1t.T, grad_w2
 
     return jax.shard_map(

time: 634 us -> 637 us (level)
  waiting for transfers between devices: 314 us -> 344 us
  Pallas kernels: 137 us -> 114 us
    all_gather x6 -> x3, waiting for transfers between devices: 134 us -> 208 us  [the longest x1 150 us: body(): lax.all_gather(jnp.concatenate(grads, axis=0), ('data', 'tensor'), axis=0...]
    reduce_scatter x2, waiting for transfers between devices: 165 us -> 100 us  [the longest x1 56.7 us: body(): lax.psum_scatter(grad_w2, 'tensor', scatter_dimension=0, tiled=True)]
    pallas_call x2 -> x1, Pallas kernels: 101 us -> 77.2 us  [scatter_rows(): pl.pallas_call(functools.partial(scatter_kernel, rows.bit_length(), n_dev...]
    reduce_scatter x2, waiting for transfers between devices: 12.9 us -> 34.7 us  [body(): lax.psum_scatter(partial_rows, 'tensor', scatter_dimension=0, tiled=True)]
  transfers between devices with their start and end apart: 10 -> 8, of which waited for: 7 -> 7; matrix products, arithmetic and copies ran while one was open for 14% -> 13% of each run, Pallas kernels for 14% -> 6%
where the time goes in v2:
time: 637 us; the launch traced here: 635 us
  waiting for transfers between devices  344 us (54%)
  Pallas kernels  114 us (18%)
  matrix products  64.7 us (10%)
  local copies, waits for them, and re-layouts  58.9 us (9%)
  other arithmetic  27.3 us (4%)
  between operations  14.5 us (2%)
  blocking collectives  12 us (2%)
    all_gather x1, waiting for transfers between devices, body(): lax.all_gather(jnp.concatenate(grads, axis=0), ('data', 'tensor'), axis=0...  150 us
    pallas_call x1, Pallas kernels, scatter_rows(): pl.pallas_call(functools.partial(scatter_kernel, rows.bit_length(), n_dev...  77.2 us
    reduce_scatter x1, waiting for transfers between devices, body(): lax.psum_scatter(grad_w2, 'tensor', scatter_dimension=0, tiled=True)  56.7 us
    gather x2, local copies, waits for them, and re-layouts, body(): picked = jnp.take(embed_table, jnp.where(is_owned, local_ids, 0), axis=0)  48.1 us
    reduce_scatter x1, waiting for transfers between devices, body(): lax.psum_scatter(grad_w1t, 'tensor', scatter_dimension=0, tiled=True)  43.4 us
    pallas_call x1, Pallas kernels, list_owned(): pl.pallas_call(functools.partial(list_kernel, rows, bits, n_tok // n_part...  36.5 us
    reduce_scatter x2, waiting for transfers between devices, body(): lax.psum_scatter(partial_rows, 'tensor', scatter_dimension=0, tiled=True)  34.7 us
    all_gather x1, waiting for transfers between devices, body(): w1t = lax.all_gather(w1t, 'tensor', axis=0, tiled=True)  31.8 us
  transfers between devices with their start and end apart: 8, of which 7 were waited for; matrix products, arithmetic and copies ran while one was open for 13% of the time, Pallas kernels for 6%

profile of v2, /device:TPU:97, one launch (start us, length us, event | category | flops | bytes accessed | tf_op | source)
XLA Modules:
  0.0 635.4 jit_solution(12226216528691882544)
XLA Ops:
  7.2 0.8 reshape.61
  8.1 24.0 %gather_fusion = bf16[4096,768]{1,0:T(8,128)(2,1)} fusion(bf16[6288,768]{1,0:T(8,128)(2,1)} %param.9, s32[4096]{0:T(1024)S(1)} %fusion.42), kind=kCustom, calls=%fused_computation.clone | custom fusion | bytes 12599296 | tf_op jit(solution)/shard_map/jit(_take)/gather | solution.py:153
  32.1 8.0 %select_select_fusion.1 = bf16[4096,768]{1,0:T(8,128)(2,1)} fusion(bf16[4096,768]{1,0:T(8,128)(2,1)} %gather_fusion, pred[4096]{0:T(1024)(128)(4,1)S(1)} %get-tuple-element.38, pred[4096]{0:T(1024)(128)(4,1)S(1)} %get-tuple-element.37), kind=kLoop, calls=%fused_computation.33 | loop fusion | flops 6291456 | bytes 12591104 | tf_op jit(solution)/shard_map/jit(_where)/select_n | solution.py:154
  40.3 0.9 copy-done.12
  41.2 1.1 copy.12
  42.4 0.7 all-gather.7.cloned.1.call-update
  43.2 24.0 %gather_fusion.1 = bf16[4096,768]{1,0:T(8,128)(2,1)} fusion(bf16[6288,768]{1,0:T(8,128)(2,1)} %param.9, s32[4096]{0:T(1024)S(1)} %fusion.43), kind=kCustom, calls=%fused_computation.1.clone | custom fusion | bytes 12599296 | tf_op jit(solution)/shard_map/jit(_take)/gather | solution.py:153
  67.3 8.0 %select_select_fusion = bf16[4096,768]{1,0:T(8,128)(2,1)} fusion(bf16[4096,768]{1,0:T(8,128)(2,1)} %gather_fusion.1, pred[4096]{0:T(1024)(128)(4,1)S(1)} %get-tuple-element.40, pred[4096]{0:T(1024)(128)(4,1)S(1)} %get-tuple-element.39), kind=kLoop, calls=%fused_computation.32 | loop fusion | flops 6291456 | bytes 12591104 | tf_op jit(solution)/shard_map/jit(_where)/select_n | solution.py:154
  75.4 0.2 reduce-scatter.9.cloned.1.call-start
  75.6 0.4 copy-done.13
  76.0 0.8 copy-done.4
  76.8 1.3 fusion.52
  78.0 5.6 reduce-scatter.5.cloned.1.call-done
  83.7 1.4 fusion.38
  85.0 1.4 fusion.32
  86.4 31.8 %all-gather.5.cloned.1.call-done = bf16[3072,768]{1,0:T(8,128)(2,1)} async-done(((bf16[384,768]{1,0:T(8,128)(2,1)}), bf16[3072,768]{1,0:T(8,128)(2,1)}) %all-gather.5.cloned.1.call-update) | async-done | bytes 4718608 | tf_op jit(solution)/shard_map/all_gather | solution.py:143
  118.2 7.6 %fusion.11 = (bf16[512,3072]{1,0:T(8,128)(2,1)}, bf16[512,3072]{1,0:T(8,128)(2,1)}) fusion(bf16[512,768]{1,0:T(8,128)(2,1)S(1)} %fusion.32, bf16[3072,768]{1,0:T(8,128)(2,1)} %all-gather.5.cloned.1.call-done), kind=kOutput, calls=%fused_computation.23 | convolution fusion | flops 2433220608 | bytes 11796480 | tf_op jit(solution)/shard_map/dot_general | solution.py:170
  125.9 25.7 %all-gather.7.cloned.1.call-done = bf16[3072,768]{1,0:T(8,128)(2,1)} async-done(((bf16[384,768]{1,0:T(8,128)(2,1)}), bf16[3072,768]{1,0:T(8,128)(2,1)}) %all-gather.7.cloned.1.call-update) | async-done | bytes 4718608 | tf_op jit(solution)/shard_map/all_gather | solution.py:144
  151.5 8.6 %fusion.7 = bf16[512,3072]{1,0:T(8,128)(2,1)S(1)} fusion(bf16[512,3072]{1,0:T(8,128)(2,1)} %get-tuple-element.48, bf16[3072,768]{1,0:T(8,128)(2,1)} %all-gather.7.cloned.1.call-done, bf16[1024,768]{1,0:T(8,128)(2,1)S(1)} %copy-done.4), kind=kOutput, calls=%fused_computation.19 | convolution fusion | flops 2448949248 | bytes 11796480 | tf_op jit(solution)/shard_map/dot_general | solution.py:173
  160.1 2.7 fusion.33
  162.9 1.3 fusion.37
  164.2 29.1 %reduce-scatter.7.cloned.1.call-done = bf16[512,768]{1,0:T(8,128)(2,1)} async-done(((bf16[4096,768]{1,0:T(8,128)(2,1)}), bf16[512,768]{1,0:T(8,128)(2,1)}) %reduce-scatter.7.cloned.1.call-update) | async-done | bytes 786448 | tf_op jit(solution)/shard_map/reduce_scatter | solution.py:155
  193.3 1.4 fusion.40
  194.7 1.5 fusion.26
  196.2 7.3 %fusion.17 = (bf16[512,3072]{1,0:T(8,128)(2,1)}, bf16[512,3072]{1,0:T(8,128)(2,1)S(1)}) fusion(bf16[512,768]{1,0:T(8,128)(2,1)S(1)} %fusion.26, bf16[3072,768]{1,0:T(8,128)(2,1)} %all-gather.5.cloned.1.call-done), kind=kOutput, calls=%fused_computation.29 | convolution fusion | flops 2433220608 | bytes 11796480 | tf_op jit(solution)/shard_map/dot_general | solution.py:170
  203.6 6.5 %fusion.4 = bf16[512,3072]{1,0:T(8,128)(2,1)S(1)} fusion(bf16[512,3072]{1,0:T(8,128)(2,1)S(1)} %get-tuple-element.44, bf16[3072,768]{1,0:T(8,128)(2,1)S(1)} %bitcast.34, bf16[1024,768]{1,0:T(8,128)(2,1)S(1)} %copy-done.4), kind=kOutput, calls=%fused_computation.16 | convolution fusion | flops 2448949248 | bytes 11796480 | tf_op jit(solution)/shard_map/dot_general | solution.py:173
  210.1 2.7 fusion.27
  212.8 1.4 fusion.31
  214.2 2.7 fusion.53
  216.9 5.4 convolution_add_fusion.1
  222.3 0.1 reduce-scatter.11.cloned.1.call-start
  222.4 1.0 copy-done.11
  223.4 4.8 fusion.54
  228.2 5.4 convolution_add_fusion
  233.7 43.4 %reduce-scatter.9.cloned.1.call-done = f32[384,768]{1,0:T(8,128)} async-done(((f32[3072,768]{1,0:T(8,128)}), f32[384,768]{1,0:T(8,128)}) %reduce-scatter.9.cloned.1.call-update) | async-done | bytes 1179664 | tf_op jit(solution)/shard_map/reduce_scatter | solution.py:190
  277.1 56.7 %reduce-scatter.11.cloned.1.call-done = f32[384,768]{1,0:T(8,128)} async-done(((f32[3072,768]{1,0:T(8,128)}), f32[384,768]{1,0:T(8,128)}) %reduce-scatter.11.cloned.1.call-update) | async-done | bytes 1179664 | tf_op jit(solution)/shard_map/reduce_scatter | solution.py:189
  333.9 1.2 pad_maximum_fusion.1
  335.2 36.5 %shard_map.93 = s32[8320]{0:T(1024)} custom-call(s32[1]{0:T(128)} %bitcast.3.base_ref, s32[8192]{0:T(1024)} %ids_ref.1), custom_call_target="tpu_custom_call" | custom-call | flops 32768000 | bytes 65536 | tf_op jit(solution)/shard_map/pallas_call | solution.py:45
  371.8 0.8 reshape.80
  372.6 12.0 %all-gather = s32[4,1,8320]{2,1,0:T(1,128)S(1)} all-gather(s32[1,1,8320]{2,1,0:T(1,128)S(1)} %reshape.80), channel_id=1, replica_groups=mesh['pod'=1,'data'=4,'tensor'=8] {'data'}, dimensions={0}, use_global_device_ids=true | all-gather | bytes 166400 | tf_op jit(solution)/shard_map/all_gather | solution.py:158
  384.5 0.3 reduce
  385.0 6.1 fusion.39
  391.1 5.0 fusion.41
  396.0 1.2 pad_maximum_fusion
  397.3 2.7 copy.13
  399.9 150.4 %all-gather.9.cloned.1.call-done.part_ref = bf16[32768,768]{1,0:T(8,128)(2,1)} async-done(((bf16[1024,768]{1,0:T(8,128)(2,1)}), bf16[32768,768]{1,0:T(8,128)(2,1)}) %all-gather.9.cloned.1.call-update) | async-done | bytes 50331664 | tf_op jit(solution)/shard_map/all_gather | solution.py:185
  550.3 77.2 %shard_map.94 = f32[6288,768]{1,0:T(8,128)} custom-call(s32[33280]{0:T(1024)S(1)} %reshape.81.list_ref, bf16[32768,768]{1,0:T(8,128)(2,1)} %all-gather.9.cloned.1.call-done.part_ref), custom_call_target="tpu_custom_call" | custom-call | flops 32768000000 | bytes 69648384 | tf_op jit(solution)/shard_map/pallas_call | solution.py:109
  627.5 1.0 copy.16
  (65 shorter events, 1.0 us)
Async XLA Ops:
  7.2 76.5 %reduce-scatter.5.cloned.1.call-start = ((), (), s32[]{:S(2)}) async-start(), calls=%async_computation.4 | async-start | bytes 7077888 | tf_op jit(solution)/shard_map/reduce_scatter | solution.py:155
  40.1 1.1 copy-start.12
  40.2 78.0 %all-gather.5.cloned.1.call-start = ((), (), s32[]{:S(2)}) async-start(), calls=%async_computation.5 | async-start | bytes 5308416 | tf_op jit(solution)/shard_map/all_gather | solution.py:143
  42.3 109.2 %all-gather.7.cloned.1.call-start = ((), (), s32[]{:S(2)}) async-start(), calls=%async_computation.6 | async-start | bytes 5308416 | tf_op jit(solution)/shard_map/all_gather | solution.py:144
  43.1 150.2 %reduce-scatter.7.cloned.1.call-start = ((), (), s32[]{:S(2)}) async-start(), calls=%async_computation.7 | async-start | bytes 7077888 | tf_op jit(solution)/shard_map/reduce_scatter | solution.py:155
  75.3 0.7 copy-start.13
  75.3 1.5 copy-start.4
  75.4 201.7 %reduce-scatter.9.cloned.1.call-start = ((), (), s32[]{:S(2)}) async-start(), calls=%async_computation.9 | async-start | bytes 10616832 | tf_op jit(solution)/shard_map/reduce_scatter | solution.py:190
  86.4 39.4 %copy-start.9 = (bf16[512,768]{1,0:T(8,128)(2,1)}, bf16[512,768]{1,0:T(8,128)(2,1)S(1)}, u32[]{:S(2)}) copy-start(bf16[512,768]{1,0:T(8,128)(2,1)S(1)} %fusion.32) | copy-start | bytes 2359300
  151.5 8.6 %copy-start = (bf16[512,768]{1,0:T(8,128)(2,1)S(1)}, bf16[512,768]{1,0:T(8,128)(2,1)}, u32[]{:S(2)}) copy-start(bf16[512,768]{1,0:T(8,128)(2,1)} %reduce-scatter.5.cloned.1.call-done) | copy-start | bytes 2359300
  151.5 8.6 %copy-start.14 = (bf16[3072,768]{1,0:T(8,128)(2,1)S(1)}, bf16[3072,768]{1,0:T(8,128)(2,1)}, u32[]{:S(2)}) copy-start(bf16[3072,768]{1,0:T(8,128)(2,1)} %all-gather.5.cloned.1.call-done) | copy-start | bytes 14155780
  160.1 2.7 copy-start.15
  194.7 8.9 %slice-start = ((s8[4718592]{0:T(1024)(128)(4,1)}), s8[4194304]{0:T(1024)(128)(4,1)S(1)}, s32[]{:S(2)}) async-start(s8[4718592]{0:T(1024)(128)(4,1)} %bitcast.33), calls=%async_computation.12 | async-start | bytes 8388608
  196.2 7.3 %slice-start.1 = ((s8[4718592]{0:T(1024)(128)(4,1)}), s8[524288]{0:T(1024)(128)(4,1)S(1)}, s32[]{:S(2)}) async-start(s8[4718592]{0:T(1024)(128)(4,1)} %bitcast.33), calls=%async_computation.13 | async-start | bytes 1048576
  196.2 13.8 %slice-start.2 = ((s8[4718592]{0:T(1024)(128)(4,1)}), s8[4194304]{0:T(1024)(128)(4,1)S(1)}, s32[]{:S(2)}) async-start(s8[4718592]{0:T(1024)(128)(4,1)} %bitcast.35), calls=%async_computation.14 | async-start | bytes 8388608
  203.5 6.5 %copy-start.1 = (bf16[512,768]{1,0:T(8,128)(2,1)S(1)}, bf16[512,768]{1,0:T(8,128)(2,1)}, u32[]{:S(2)}) copy-start(bf16[512,768]{1,0:T(8,128)(2,1)} %reduce-scatter.7.cloned.1.call-done) | copy-start | bytes 2359300
  203.5 6.5 %slice-start.3 = ((s8[4718592]{0:T(1024)(128)(4,1)}), s8[524288]{0:T(1024)(128)(4,1)S(1)}, s32[]{:S(2)}) async-start(s8[4718592]{0:T(1024)(128)(4,1)} %bitcast.35), calls=%async_computation.15 | async-start | bytes 1048576
  210.1 4.1 copy-start.10
  210.1 4.1 copy-start.16
  222.3 1.1 copy-start.11
  222.3 5.9 copy-start.7
  222.3 111.4 %reduce-scatter.11.cloned.1.call-start = ((), (), s32[]{:S(2)}) async-start(), calls=%async_computation.10 | async-start | bytes 10616832 | tf_op jit(solution)/shard_map/reduce_scatter | solution.py:189
  223.4 4.8 copy-start.2
  233.6 100.3 %copy-start.5 = (bf16[512,768]{1,0:T(8,128)(2,1)S(1)}, bf16[512,768]{1,0:T(8,128)(2,1)}, u32[]{:S(2)}) copy-start(bf16[512,768]{1,0:T(8,128)(2,1)} %fusion.37) | copy-start | bytes 2359300
  233.6 100.4 %copy-start.6 = (bf16[512,768]{1,0:T(8,128)(2,1)S(1)}, bf16[512,768]{1,0:T(8,128)(2,1)}, u32[]{:S(2)}) copy-start(bf16[512,768]{1,0:T(8,128)(2,1)} %fusion.31) | copy-start | bytes 2359300
  233.6 163.7 %all-reduce.3.cloned.1.call-start = ((), (), s32[]{:S(2)}) async-start(), calls=%async_computation.11 | async-start | bytes 4718592 | tf_op jit(solution)/shard_map/psum | solution.py:191
  333.8 216.5 %all-gather.9.cloned.1.call-start = ((), (), s32[]{:S(2)}) async-start(), calls=%async_computation.8 | async-start | bytes 51904512 | tf_op jit(solution)/shard_map/all_gather | solution.py:185
  385.0 6.1 copy-start.3
  399.9 227.6 %copy-start.8 = (f32[384,768]{1,0:T(8,128)S(1)}, f32[384,768]{1,0:T(8,128)}, u32[]{:S(2)}) copy-start(f32[384,768]{1,0:T(8,128)} %get-tuple-element.52) | copy-start | bytes 3538948
Sparse Core Ops, SparseCore 0:
  40.3 43.3 reduce-scatter.4
  85.8 32.3 all-gather.4
  119.8 31.6 all-gather.6
  154.3 38.9 reduce-scatter.6
  222.5 54.6 reduce-scatter.8
  279.3 54.4 reduce-scatter.10
  336.2 58.9 all-reduce.2
  397.9 152.4 all-gather.8

commit v3 on v2

--- a/solution.py
+++ b/solution.py
@@ -127,21 +127,84 @@
     )(lists, part)
 
 
+def sum_kernel(n, part_ref, out_ref, parts, mine, sums, send_parts, recv_parts, send_sums, recv_sums):
+    me = lax.axis_index("data")
+    rows = part_ref.shape[0] // n
+    peers = [lax.rem(me + k, n) for k in range(1, n)]
+
+    barrier = pltpu.get_barrier_semaphore()
+    for peer in peers:
+        pl.semaphore_signal(barrier, inc=1, device_id={"data": peer}, device_id_type=pl.DeviceIdType.MESH)
+    pl.semaphore_wait(barrier, n - 1)
+
+    def piece(of):
+        return pl.ds(pl.multiple_of(of * rows, 8), rows)
+
+    def send(src, slots, k, send_sem, recv_sem):
+        copy = pltpu.make_async_remote_copy(
+            src_ref=src,
+            dst_ref=slots.at[k],
+            send_sem=send_sem.at[k],
+            recv_sem=recv_sem.at[k],
+            device_id={"data": peers[k]},
+            device_id_type=pl.DeviceIdType.MESH,
+        )
+        copy.start()
+        return copy
+
+    first = [send(part_ref.at[piece(peers[k])], parts, k, send_parts, recv_parts) for k in range(n - 1)]
+    total = part_ref[piece(me), :]
+    for k in range(n - 1):
+        first[k].wait()
+        total = total + parts[k]
+    mine[...] = total
+    out_ref[piece(me), :] = mine[...]
+    second = [send(mine, sums, k, send_sums, recv_sums) for k in range(n - 1)]
+    for k in range(n - 1):
+        second[k].wait()
+        out_ref[piece(lax.rem(me + n - 1 - k, n)), :] = sums[k]
+
+
+def sum_over_data(part, n, number):
+    rows, dim = part.shape[0] // n, part.shape[1]
+    sems = pltpu.SemaphoreType.DMA((n - 1,))
+    return pl.pallas_call(
+        functools.partial(sum_kernel, n),
+        out_shape=jax.ShapeDtypeStruct(part.shape, F32),
+        in_specs=[pl.BlockSpec(memory_space=pltpu.VMEM)],
+        out_specs=pl.BlockSpec(memory_space=pltpu.VMEM),
+        scratch_shapes=[
+            pltpu.VMEM((n - 1, rows, dim), F32),
+            pltpu.VMEM((rows, dim), F32),
+            pltpu.VMEM((n - 1, rows, dim), F32),
+            sems,
+            sems,
+            sems,
+            sems,
+        ],
+        compiler_params=pltpu.CompilerParams(collective_id=number, has_side_effects=True, vmem_limit_bytes=16 << 20),
+        cost_estimate=pl.CostEstimate(flops=part.size * 50000, bytes_accessed=8 * part.size, transcendentals=0),
+    )(part)
+
+
 def solution(mesh):
     tok_spec = P(("pod", "data", "tensor"), None)
     n_dev = mesh.shape["tensor"]
     n_rep = mesh.shape["data"]
 
     def body(token_ids, embed_table, norm_gain, w_in, w_out, d_out):
-        shard_rows, _ = embed_table.shape
+        shard_rows, dim = embed_table.shape
         rank = lax.axis_index("tensor")
         n_tok = token_ids.shape[0]
         per_dev = n_tok // n_dev
         half = per_dev // HALVES
 
-        w1t = with_layout_constraint(w_in.T, Layout(major_to_minor=(0, 1)))
-        w1t = lax.all_gather(w1t, "tensor", axis=0, tiled=True)
-        w2 = lax.all_gather(w_out, "tensor", axis=0, tiled=True)
+        cols = w_out.shape[0]
+        w_both = jnp.concatenate([w_in.T, w_out], axis=0)
+        w_both = with_layout_constraint(w_both, Layout(major_to_minor=(0, 1)))
+        w_both = lax.all_gather(w_both, "tensor", axis=0)
+        w1t = lax.optimization_barrier(w_both[:, :cols].reshape(-1, dim))
+        w2 = lax.optimization_barrier(w_both[:, cols:].reshape(-1, dim))
 
         ids_by_dev = token_ids.reshape(n_dev, HALVES, half)
         gain_f32 = norm_gain.astype(F32)
@@ -159,18 +222,19 @@
 
         outs, grads, saved = [], [], []
         for k in range(HALVES):
+            d_half = lax.slice_in_dim(d_out, k * half, (k + 1) * half)
+            grad_hidden = lax.dot_general(d_half, w2, NT, preferred_element_type=F32)
+            grad_hidden = lax.optimization_barrier(grad_hidden)
             x_half = x_halves[k]
             if k > 0:
                 x_half, _ = lax.optimization_barrier((x_half, d_embed))
             x_f32 = x_half.astype(F32)
-            d_half = lax.slice_in_dim(d_out, k * half, (k + 1) * half)
             inv_rms = lax.rsqrt(jnp.mean(x_f32 * x_f32, axis=-1, keepdims=True) + NORM_EPS)
             x_hat = x_f32 * inv_rms
             normed = (x_hat * gain_f32).astype(BF16)
             pre_gelu = lax.dot_general(normed, w1t, NT, preferred_element_type=F32).astype(BF16)
             hidden_f32, gelu_pull = jax.vjp(gelu_tanh, pre_gelu.astype(F32))
             hidden = hidden_f32.astype(BF16)
-            grad_hidden = lax.dot_general(d_half, w2, NT, preferred_element_type=F32)
             grad_pre = gelu_pull(grad_hidden)[0].astype(BF16)
             d_normed = jnp.dot(grad_pre, w1t, preferred_element_type=F32)
             d_hat = d_normed * gain_f32
@@ -188,7 +252,8 @@
         grad_w1t = sum(lax.dot_general(u, n, TN, preferred_element_type=F32) for n, _, u, _ in saved)
         grad_w2 = lax.psum_scatter(grad_w2, "tensor", scatter_dimension=0, tiled=True)
         grad_w1t = lax.psum_scatter(grad_w1t, "tensor", scatter_dimension=0, tiled=True)
-        grad_w2, grad_w1t = lax.psum((grad_w2, grad_w1t), "data")
+        grad_w2 = sum_over_data(grad_w2, n_rep, 0)
+        grad_w1t = sum_over_data(grad_w1t, n_rep, 1)
         grad_table = scatter_rows(lists, grad_all, shard_rows, n_dev, n_rep)
         return block_out, grad_table, grad_w1t.T, grad_w2
 

time: 637 us -> 581 us (0.912)
  waiting for transfers between devices: 344 us -> 201 us
  Pallas kernels: 114 us -> 189 us
  local copies, waits for them, and re-layouts: 58.9 us -> 69.1 us
    pallas_call x0 -> x2, Pallas kernels: none -> 75.4 us  [sum_over_data(): pl.pallas_call(functools.partial(sum_kernel, n), out_shape=jax.ShapeDtype...]
    reduce_scatter x1, waiting for transfers between devices: 56.7 us -> 0.01 us  [body(): lax.psum_scatter(grad_w2, 'tensor', scatter_dimension=0, tiled=True)]
    reduce_scatter x1, waiting for transfers between devices: 43.4 us -> 6.84 us  [body(): lax.psum_scatter(grad_w1t, 'tensor', scatter_dimension=0, tiled=True)]
    all_gather x1, waiting for transfers between devices: 150 us -> 122 us  [body(): lax.all_gather(jnp.concatenate(grads, axis=0), ('data', 'tensor'), axis=0...]
    reduce_scatter x2, waiting for transfers between devices: 34.7 us -> 20.9 us  [body(): lax.psum_scatter(partial_rows, 'tensor', scatter_dimension=0, tiled=True)]
    dot_general x2, matrix products: 15 us -> 7.18 us  [body(): grad_hidden = lax.dot_general(d_half, w2, NT, preferred_element_type=F32)]
    slice x0 -> x1, local copies, waits for them, and re-layouts: none -> 6.72 us  [body(): w2 = lax.optimization_barrier(w_both[:, cols:].reshape(-1, dim))]
    all_gather x2 -> x1, waiting for transfers between devices: 57.4 us -> 51.6 us  [body(): w_both = lax.all_gather(w_both, 'tensor', axis=0)]
  transfers between devices with their start and end apart: 8 -> 6, of which waited for: 7 -> 5; matrix products, arithmetic and copies ran while one was open for 13% -> 16% of each run, Pallas kernels for 6% -> 19%
where the time goes in v3:
time: 581 us; the launch traced here: 575 us
  waiting for transfers between devices  201 us (35%)
  Pallas kernels  189 us (33%)
  local copies, waits for them, and re-layouts  69.1 us (12%)
  matrix products  61.2 us (11%)
  other arithmetic  28.3 us (5%)
  between operations  14.7 us (3%)
  blocking collectives  10 us (2%)
    all_gather x1, waiting for transfers between devices, body(): lax.all_gather(jnp.concatenate(grads, axis=0), ('data', 'tensor'), axis=0...  122 us
    pallas_call x1, Pallas kernels, scatter_rows(): pl.pallas_call(functools.partial(scatter_kernel, rows.bit_length(), n_dev...  77.2 us
    pallas_call x2, Pallas kernels, sum_over_data(): pl.pallas_call(functools.partial(sum_kernel, n), out_shape=jax.ShapeDtype...  75.4 us
    all_gather x1, waiting for transfers between devices, body(): w_both = lax.all_gather(w_both, 'tensor', axis=0)  51.6 us
    gather x2, local copies, waits for them, and re-layouts, body(): picked = jnp.take(embed_table, jnp.where(is_owned, local_ids, 0), axis=0)  48.1 us
    pallas_call x1, Pallas kernels, list_owned(): pl.pallas_call(functools.partial(list_kernel, rows, bits, n_tok // n_part...  36.5 us
    reduce_scatter x2, waiting for transfers between devices, body(): lax.psum_scatter(partial_rows, 'tensor', scatter_dimension=0, tiled=True)  20.9 us
    dot_general x2, matrix products, body(): lax.dot_general(normed, w1t, NT, preferred_element_type=F32).astype(BF16)  18.5 us
  transfers between devices with their start and end apart: 6, of which 5 were waited for; matrix products, arithmetic and copies ran while one was open for 16% of the time, Pallas kernels for 19%

profile of v3, /device:TPU:97, one launch (start us, length us, event | category | flops | bytes accessed | tf_op | source)
XLA Modules:
  0.0 574.7 jit_solution(7378185940425758372)
XLA Ops:
  7.2 0.8 reshape.67
  8.1 24.0 %gather_fusion = bf16[4096,768]{1,0:T(8,128)(2,1)} fusion(bf16[6288,768]{1,0:T(8,128)(2,1)} %param.9, s32[4096]{0:T(1024)S(1)} %fusion.42), kind=kCustom, calls=%fused_computation.clone | custom fusion | bytes 12599296 | tf_op jit(solution)/shard_map/jit(_take)/gather | solution.py:216
  32.1 8.0 %select_select_fusion.1 = bf16[4096,768]{1,0:T(8,128)(2,1)} fusion(bf16[4096,768]{1,0:T(8,128)(2,1)} %gather_fusion, pred[4096]{0:T(1024)(128)(4,1)S(1)} %get-tuple-element.42, pred[4096]{0:T(1024)(128)(4,1)S(1)} %get-tuple-element.41), kind=kLoop, calls=%fused_computation.33 | loop fusion | flops 6291456 | bytes 12591104 | tf_op jit(solution)/shard_map/jit(_where)/select_n | solution.py:217
  40.2 0.9 copy-done.18
  41.4 1.1 pad_maximum_fusion.2
  42.7 24.0 %gather_fusion.1 = bf16[4096,768]{1,0:T(8,128)(2,1)} fusion(bf16[6288,768]{1,0:T(8,128)(2,1)} %param.9, s32[4096]{0:T(1024)S(1)} %fusion.43), kind=kCustom, calls=%fused_computation.1.clone | custom fusion | bytes 12599296 | tf_op jit(solution)/shard_map/jit(_take)/gather | solution.py:216
  66.7 8.0 %select_select_fusion = bf16[4096,768]{1,0:T(8,128)(2,1)} fusion(bf16[4096,768]{1,0:T(8,128)(2,1)} %gather_fusion.1, pred[4096]{0:T(1024)(128)(4,1)S(1)} %get-tuple-element.44, pred[4096]{0:T(1024)(128)(4,1)S(1)} %get-tuple-element.43), kind=kLoop, calls=%fused_computation.32 | loop fusion | flops 6291456 | bytes 12591104 | tf_op jit(solution)/shard_map/jit(_where)/select_n | solution.py:217
  75.5 0.8 copy-done.7
  76.2 1.2 fusion.47
  77.5 6.2 %reduce-scatter.5.cloned.1.call-done = bf16[512,768]{1,0:T(8,128)(2,1)} async-done(((bf16[4096,768]{1,0:T(8,128)(2,1)}), bf16[512,768]{1,0:T(8,128)(2,1)}) %reduce-scatter.5.cloned.1.call-update) | async-done | bytes 786448 | tf_op jit(solution)/shard_map/reduce_scatter | solution.py:218
  83.6 1.4 fusion.38
  85.0 1.4 fusion.32
  86.4 51.6 %all-gather.7.cloned.1.call-done = bf16[6144,768]{1,0:T(8,128)(2,1)} async-done(((bf16[768,768]{1,0:T(8,128)(2,1)}), bf16[6144,768]{1,0:T(8,128)(2,1)}) %all-gather.7.cloned.1.call-update) | async-done | bytes 9437200 | tf_op jit(solution)/shard_map/all_gather | solution.py:205
  138.0 6.7 %fusion.46 = (bf16[8,384,768]{2,1,0:T(8,128)(2,1)S(1)}, bf16[8,384,768]{2,1,0:T(8,128)(2,1)}) fusion(bf16[8,768,768]{2,1,0:T(8,128)(2,1)} %bitcast.35), kind=kLoop, calls=%fused_computation.89 | loop fusion | bytes 18874368 | tf_op jit(solution)/shard_map/slice | solution.py:207
  144.7 2.6 convolution_bitcast_fusion.1
  147.4 1.6 copy-done.9
  149.0 7.8 %fusion.11 = (bf16[512,3072]{1,0:T(8,128)(2,1)}, bf16[512,3072]{1,0:T(8,128)(2,1)S(1)}) fusion(f32[512,3072]{1,0:T(8,128)S(1)} %convolution_bitcast_fusion.1, bf16[512,768]{1,0:T(8,128)(2,1)S(1)} %fusion.32, bf16[3072,768]{1,0:T(8,128)(2,1)S(1)} %bitcast.41), kind=kOutput, calls=%fused_computation.23 | convolution fusion | flops 2453667840 | bytes 18087936 | tf_op jit(solution)/shard_map/dot_general | solution.py:235
  156.8 2.7 fusion.33
  159.5 1.3 fusion.37
  160.8 4.5 convolution_bitcast_fusion
  165.4 14.8 %reduce-scatter.7.cloned.1.call-done = bf16[512,768]{1,0:T(8,128)(2,1)} async-done(((bf16[4096,768]{1,0:T(8,128)(2,1)}), bf16[512,768]{1,0:T(8,128)(2,1)}) %reduce-scatter.7.cloned.1.call-update) | async-done | bytes 786448 | tf_op jit(solution)/shard_map/reduce_scatter | solution.py:218
  180.2 1.4 fusion.40
  181.5 1.5 fusion.26
  183.1 10.7 %fusion.4 = (bf16[512,3072]{1,0:T(8,128)(2,1)S(1)}, bf16[512,3072]{1,0:T(8,128)(2,1)S(1)}) fusion(f32[512,3072]{1,0:T(8,128)} %convolution_bitcast_fusion, bf16[512,768]{1,0:T(8,128)(2,1)S(1)} %fusion.26, bf16[3072,768]{1,0:T(8,128)(2,1)} %bitcast.40), kind=kOutput, calls=%fused_computation.16 | convolution fusion | flops 2453667840 | bytes 18087936 | tf_op jit(solution)/shard_map/dot_general | solution.py:235
  193.9 2.8 fusion.27
  196.7 1.3 fusion.31
  198.5 2.7 fusion.49
  201.3 5.3 convolution_add_fusion
  206.7 1.0 copy-done.16
  207.7 4.8 fusion.48
  212.5 5.4 convolution_add_fusion.1
  218.0 1.0 copy-done.10
  219.3 1.3 pad_maximum_fusion.1
  220.6 36.5 %shard_map.93 = s32[8320]{0:T(1024)} custom-call(s32[1]{0:T(128)} %bitcast.8.base_ref, s32[8192]{0:T(1024)} %ids_ref.1), custom_call_target="tpu_custom_call" | custom-call | flops 32768000 | bytes 65536 | tf_op jit(solution)/shard_map/pallas_call | solution.py:45
  257.1 0.8 reshape.89
  257.9 10.0 %all-gather.1 = s32[4,1,8320]{2,1,0:T(1,128)S(1)} all-gather(s32[1,1,8320]{2,1,0:T(1,128)S(1)} %reshape.89), channel_id=1, replica_groups=mesh['pod'=1,'data'=4,'tensor'=8] {'data'}, dimensions={0}, use_global_device_ids=true | all-gather | bytes 166400 | tf_op jit(solution)/shard_map/all_gather | solution.py:221
  268.4 6.9 %fusion.41 = bf16[512,768]{1,0:T(8,128)(2,1)S(1)} fusion(bf16[512,768]{1,0:T(8,128)(2,1)S(1)} %copy-done.3, bf16[512,3072]{1,0:T(8,128)(2,1)} %copy-done.4, bf16[3072,768]{1,0:T(8,128)(2,1)} %bitcast.38), kind=kOutput, calls=%fused_computation.67 | convolution fusion | flops 2417098752 | bytes 9437184 | tf_op jit(solution)/shard_map/dot_general | solution.py:246
  275.3 5.1 fusion.39
  280.4 1.2 pad_maximum_fusion
  281.6 1.3 copy-done
  282.9 28.9 %shard_map.96 = f32[384,768]{1,0:T(8,128)S(1)} custom-call(f32[384,768]{1,0:T(8,128)S(1)} %copy-done), custom_call_target="tpu_custom_call" | custom-call | flops 14745600000 | bytes 2359296 | tf_op jit(solution)/shard_map/pallas_call | solution.py:171
  311.8 6.8 %reduce-scatter.9.cloned.1.call-done.part_ref = f32[384,768]{1,0:T(8,128)} async-done(((f32[3072,768]{1,0:T(8,128)}), f32[384,768]{1,0:T(8,128)}) %reduce-scatter.9.cloned.1.call-update) | async-done | bytes 1179664 | tf_op jit(solution)/shard_map/reduce_scatter | solution.py:254
  318.7 1.3 copy-done.1
  320.0 46.5 %shard_map.95 = f32[384,768]{1,0:T(8,128)S(1)} custom-call(f32[384,768]{1,0:T(8,128)S(1)} %copy-done.1), custom_call_target="tpu_custom_call" | custom-call | flops 14745600000 | bytes 2359296 | tf_op jit(solution)/shard_map/pallas_call | solution.py:171
  366.5 1.4 copy.17
  367.9 121.5 %all-gather.5.cloned.1.call-done.part_ref = bf16[32768,768]{1,0:T(8,128)(2,1)} async-done(((bf16[1024,768]{1,0:T(8,128)(2,1)}), bf16[32768,768]{1,0:T(8,128)(2,1)}) %all-gather.5.cloned.1.call-update) | async-done | bytes 50331664 | tf_op jit(solution)/shard_map/all_gather | solution.py:249
  489.4 77.2 %shard_map.94 = f32[6288,768]{1,0:T(8,128)} custom-call(s32[33280]{0:T(1024)S(1)} %reshape.90.list_ref, bf16[32768,768]{1,0:T(8,128)(2,1)} %all-gather.5.cloned.1.call-done.part_ref), custom_call_target="tpu_custom_call" | custom-call | flops 32768000000 | bytes 69648384 | tf_op jit(solution)/shard_map/pallas_call | solution.py:109
  566.6 1.0 copy.21
  (72 shorter events, 2.9 us)
Async XLA Ops:
  7.2 76.5 %reduce-scatter.5.cloned.1.call-start = ((), (), s32[]{:S(2)}) async-start(), calls=%async_computation.4 | async-start | bytes 7077888 | tf_op jit(solution)/shard_map/reduce_scatter | solution.py:218
  40.1 1.1 copy-start.18
  40.1 1.3 copy-start.19
  40.2 97.9 %all-gather.7.cloned.1.call-start = ((), (), s32[]{:S(2)}) async-start(), calls=%async_computation.9 | async-start | bytes 10616832 | tf_op jit(solution)/shard_map/all_gather | solution.py:205
  42.6 137.6 %reduce-scatter.7.cloned.1.call-start = ((), (), s32[]{:S(2)}) async-start(), calls=%async_computation.5 | async-start | bytes 7077888 | tf_op jit(solution)/shard_map/reduce_scatter | solution.py:218
  74.8 0.7 copy-start.20
  74.8 1.5 copy-start.7
  74.8 206.8 %reduce-scatter.11.cloned.1.call-start = ((), (), s32[]{:S(2)}) async-start(), calls=%async_computation.8 | async-start | bytes 10616832 | tf_op jit(solution)/shard_map/reduce_scatter | solution.py:253
  86.4 61.0 %copy-start.15 = (bf16[512,768]{1,0:T(8,128)(2,1)}, bf16[512,768]{1,0:T(8,128)(2,1)S(1)}, u32[]{:S(2)}) copy-start(bf16[512,768]{1,0:T(8,128)(2,1)S(1)} %fusion.32) | copy-start | bytes 2359300
  144.7 16.1 %copy-start.8 = (bf16[8,384,768]{2,1,0:T(8,128)(2,1)}, bf16[8,384,768]{2,1,0:T(8,128)(2,1)S(1)}, u32[]{:S(2)}) copy-start(bf16[8,384,768]{2,1,0:T(8,128)(2,1)S(1)} %get-tuple-element.31) | copy-start | bytes 14155780
  144.7 4.2 copy-start.9
  149.0 7.8 %copy-start.2 = (bf16[512,768]{1,0:T(8,128)(2,1)S(1)}, bf16[512,768]{1,0:T(8,128)(2,1)}, u32[]{:S(2)}) copy-start(bf16[512,768]{1,0:T(8,128)(2,1)} %reduce-scatter.5.cloned.1.call-done) | copy-start | bytes 2359300
  156.8 2.7 copy-start.23
  181.5 12.3 %slice-start = ((s8[4718592]{0:T(1024)(128)(4,1)}), s8[4194304]{0:T(1024)(128)(4,1)S(1)}, s32[]{:S(2)}) async-start(s8[4718592]{0:T(1024)(128)(4,1)} %bitcast.43), calls=%async_computation.10 | async-start | bytes 8388608
  183.1 10.7 %copy-start.12 = (bf16[512,768]{1,0:T(8,128)(2,1)}, bf16[512,768]{1,0:T(8,128)(2,1)S(1)}, u32[]{:S(2)}) copy-start(bf16[512,768]{1,0:T(8,128)(2,1)S(1)} %fusion.26) | copy-start | bytes 2359300
  183.1 10.8 %copy-start.3 = (bf16[512,768]{1,0:T(8,128)(2,1)S(1)}, bf16[512,768]{1,0:T(8,128)(2,1)}, u32[]{:S(2)}) copy-start(bf16[512,768]{1,0:T(8,128)(2,1)} %reduce-scatter.7.cloned.1.call-done) | copy-start | bytes 2359300
  183.1 10.8 %slice-start.1 = ((s8[4718592]{0:T(1024)(128)(4,1)}), s8[524288]{0:T(1024)(128)(4,1)S(1)}, s32[]{:S(2)}) async-start(s8[4718592]{0:T(1024)(128)(4,1)} %bitcast.43), calls=%async_computation.11 | async-start | bytes 1048576
  193.8 2.8 copy-start.5
  193.8 7.4 %copy-start.4 = (bf16[512,3072]{1,0:T(8,128)(2,1)}, bf16[512,3072]{1,0:T(8,128)(2,1)S(1)}, u32[]{:S(2)}) copy-start(bf16[512,3072]{1,0:T(8,128)(2,1)S(1)} %get-tuple-element.16) | copy-start | bytes 9437188
  193.9 4.1 copy-start.17
  193.9 4.6 copy-start.21
  198.5 2.7 copy-start.14
  206.6 1.1 copy-start.16
  206.6 5.9 %copy-start.13 = (bf16[512,768]{1,0:T(8,128)(2,1)S(1)}, bf16[512,768]{1,0:T(8,128)(2,1)}, u32[]{:S(2)}) copy-start(bf16[512,768]{1,0:T(8,128)(2,1)} %copy-done.12) | copy-start | bytes 2359300
  206.6 112.1 %reduce-scatter.9.cloned.1.call-start = ((), (), s32[]{:S(2)}) async-start(), calls=%async_computation.7 | async-start | bytes 10616832 | tf_op jit(solution)/shard_map/reduce_scatter | solution.py:254
  207.7 4.8 copy-start.6
  217.9 1.2 copy-start.10
  217.9 1.4 copy-start.11
  217.9 271.5 %all-gather.5.cloned.1.call-start = ((), (), s32[]{:S(2)}) async-start(), calls=%async_computation.6 | async-start | bytes 51904512 | tf_op jit(solution)/shard_map/all_gather | solution.py:249
  268.4 6.9 %copy-start.22 = (bf16[512,3072]{1,0:T(8,128)(2,1)S(1)}, bf16[512,3072]{1,0:T(8,128)(2,1)}, u32[]{:S(2)}) copy-start(bf16[512,3072]{1,0:T(8,128)(2,1)} %get-tuple-element.14) | copy-start | bytes 9437188
  281.6 1.3 copy-start
  318.7 1.3 copy-start.1
Sparse Core Ops, SparseCore 0:
  40.3 43.3 reduce-scatter.4
  85.8 52.1 all-gather.6
  140.9 39.1 reduce-scatter.6
  206.7 54.6 reduce-scatter.10
  264.2 54.4 reduce-scatter.8
  320.6 168.7 all-gather.4

commit v4 on v3

--- a/solution.py
+++ b/solution.py
@@ -9,7 +9,8 @@
 from jax.sharding import PartitionSpec as P
 
 NORM_EPS = 1e-6
-HALVES = 2
+SPLIT = (5, 3)
+PAIR_ROWS = 32
 F32 = jnp.float32
 BF16 = jnp.bfloat16
 NT = (((1,), (1,)), ((), ()))
@@ -187,6 +188,56 @@
     )(part)
 
 
+def pair_kernel(blocks_ref, out_ref, recv, send_sem, recv_sem):
+    me = lax.axis_index("tensor")
+    parity = lax.rem(me, 2)
+    partner = me + 1 - 2 * parity
+    n_out, rows, _ = out_ref.shape
+
+    barrier = pltpu.get_barrier_semaphore()
+    pl.semaphore_signal(barrier, inc=1, device_id={"tensor": partner}, device_id_type=pl.DeviceIdType.MESH)
+    pl.semaphore_wait(barrier, 1)
+
+    copies = []
+    for k in range(n_out):
+        copy = pltpu.make_async_remote_copy(
+            src_ref=blocks_ref.at[2 * k + 1 - parity],
+            dst_ref=recv.at[k],
+            send_sem=send_sem.at[k],
+            recv_sem=recv_sem.at[k],
+            device_id={"tensor": partner},
+            device_id_type=pl.DeviceIdType.MESH,
+        )
+        copy.start()
+        copies.append(copy)
+    for k in range(n_out):
+        copies[k].wait()
+
+        def add(i, carry, k=k):
+            part = pl.ds(pl.multiple_of(i * PAIR_ROWS, PAIR_ROWS), PAIR_ROWS)
+            mine = blocks_ref[2 * k + parity, part, :].astype(F32)
+            out_ref[k, part, :] = (mine + recv[k, part, :].astype(F32)).astype(out_ref.dtype)
+            return carry
+
+        lax.fori_loop(0, rows // PAIR_ROWS, add, 0)
+
+
+def sum_pairs(value, n_blocks, number):
+    total, dim = value.shape
+    n_out, rows = n_blocks // 2, total // n_blocks
+    sems = pltpu.SemaphoreType.DMA((n_out,))
+    out = pl.pallas_call(
+        pair_kernel,
+        out_shape=jax.ShapeDtypeStruct((n_out, rows, dim), value.dtype),
+        in_specs=[pl.BlockSpec(memory_space=pltpu.VMEM)],
+        out_specs=pl.BlockSpec(memory_space=pltpu.VMEM),
+        scratch_shapes=[pltpu.VMEM((n_out, rows, dim), value.dtype), sems, sems],
+        compiler_params=pltpu.CompilerParams(collective_id=number, has_side_effects=True, vmem_limit_bytes=32 << 20),
+        cost_estimate=pl.CostEstimate(flops=value.size * 4000, bytes_accessed=6 * value.size, transcendentals=0),
+    )(value.reshape(n_blocks, rows, dim))
+    return out.reshape(n_out * rows, dim)
+
+
 def solution(mesh):
     tok_spec = P(("pod", "data", "tensor"), None)
     n_dev = mesh.shape["tensor"]
@@ -197,7 +248,7 @@
         rank = lax.axis_index("tensor")
         n_tok = token_ids.shape[0]
         per_dev = n_tok // n_dev
-        half = per_dev // HALVES
+        bounds = [0, per_dev * SPLIT[0] // sum(SPLIT), per_dev]
 
         cols = w_out.shape[0]
         w_both = jnp.concatenate([w_in.T, w_out], axis=0)
@@ -206,23 +257,27 @@
         w1t = lax.optimization_barrier(w_both[:, :cols].reshape(-1, dim))
         w2 = lax.optimization_barrier(w_both[:, cols:].reshape(-1, dim))
 
-        ids_by_dev = token_ids.reshape(n_dev, HALVES, half)
+        ids_by_dev = token_ids.reshape(n_dev, per_dev)
         gain_f32 = norm_gain.astype(F32)
 
         x_halves = []
-        for k in range(HALVES):
-            local_ids = ids_by_dev[:, k].reshape(-1) - rank * shard_rows
+        groups = [list(range(k, n_dev, 2)) for k in range(2)]
+        for k in range(len(SPLIT)):
+            local_ids = ids_by_dev[:, bounds[k] : bounds[k + 1]].reshape(-1) - rank * shard_rows
             is_owned = (local_ids >= 0) & (local_ids < shard_rows)
             picked = jnp.take(embed_table, jnp.where(is_owned, local_ids, 0), axis=0)
             partial_rows = jnp.where(is_owned[:, None], picked, jnp.zeros_like(picked))
-            x_halves.append(lax.psum_scatter(partial_rows, "tensor", scatter_dimension=0, tiled=True))
+            partial_rows = sum_pairs(partial_rows, n_dev, 2 + k)
+            x_halves.append(
+                lax.psum_scatter(partial_rows, "tensor", scatter_dimension=0, axis_index_groups=groups, tiled=True)
+            )
 
         lists = list_owned(token_ids, shard_rows, rank, n_dev)
         lists = lax.all_gather(lists, "data", axis=0, tiled=True)
 
-        outs, grads, saved = [], [], []
-        for k in range(HALVES):
-            d_half = lax.slice_in_dim(d_out, k * half, (k + 1) * half)
+        grads, saved = [], []
+        for k in range(len(SPLIT)):
+            d_half = lax.slice_in_dim(d_out, bounds[k], bounds[k + 1])
             grad_hidden = lax.dot_general(d_half, w2, NT, preferred_element_type=F32)
             grad_hidden = lax.optimization_barrier(grad_hidden)
             x_half = x_halves[k]
@@ -241,17 +296,20 @@
             d_norm_in = inv_rms * (d_hat - x_hat * jnp.mean(d_hat * x_hat, axis=-1, keepdims=True))
             d_embed = (d_half.astype(F32) + d_norm_in).astype(BF16)
             grads.append(d_embed)
-            normed, hidden, grad_pre, d_half, _ = lax.optimization_barrier((normed, hidden, grad_pre, d_half, d_embed))
-            saved.append((normed, hidden, grad_pre, d_half))
-            mlp_out = jnp.dot(hidden, w2, preferred_element_type=F32)
-            outs.append((x_f32 + mlp_out).astype(BF16))
-        block_out = jnp.concatenate(outs, axis=0)
+            normed, hidden, grad_pre, _ = lax.optimization_barrier((normed, hidden, grad_pre, d_embed))
+            saved.append((normed, hidden, grad_pre))
+        normed, hidden, grad_pre = (lax.optimization_barrier(jnp.concatenate(v, axis=0)) for v in zip(*saved))
+        x_f32 = jnp.concatenate(x_halves, axis=0).astype(F32)
+        mlp_out = jnp.dot(hidden, w2, preferred_element_type=F32)
+        block_out = (x_f32 + mlp_out).astype(BF16)
         grad_all = lax.all_gather(jnp.concatenate(grads, axis=0), ("data", "tensor"), axis=0, tiled=True)
 
-        grad_w2 = sum(lax.dot_general(h, d, TN, preferred_element_type=F32) for _, h, _, d in saved)
-        grad_w1t = sum(lax.dot_general(u, n, TN, preferred_element_type=F32) for n, _, u, _ in saved)
-        grad_w2 = lax.psum_scatter(grad_w2, "tensor", scatter_dimension=0, tiled=True)
-        grad_w1t = lax.psum_scatter(grad_w1t, "tensor", scatter_dimension=0, tiled=True)
+        grad_w2 = lax.dot_general(hidden, d_out, TN, preferred_element_type=F32)
+        grad_w1t = lax.dot_general(grad_pre, normed, TN, preferred_element_type=F32)
+        grad_w2 = sum_pairs(grad_w2, n_dev, 4)
+        grad_w1t = sum_pairs(grad_w1t, n_dev, 5)
+        grad_w2 = lax.psum_scatter(grad_w2, "tensor", scatter_dimension=0, axis_index_groups=groups, tiled=True)
+        grad_w1t = lax.psum_scatter(grad_w1t, "tensor", scatter_dimension=0, axis_index_groups=groups, tiled=True)
         grad_w2 = sum_over_data(grad_w2, n_rep, 0)
         grad_w1t = sum_over_data(grad_w1t, n_rep, 1)
         grad_table = scatter_rows(lists, grad_all, shard_rows, n_dev, n_rep)

time: 581 us -> 531 us (0.914)
  waiting for transfers between devices: 201 us -> 99.8 us
  Pallas kernels: 189 us -> 251 us
    all_gather x1, waiting for transfers between devices: 122 us -> 35.8 us  [body(): lax.all_gather(jnp.concatenate(grads, axis=0), ('data', 'tensor'), axis=0...]
    all_gather x1, waiting for transfers between devices: 51.6 us -> 10.6 us  [body(): w_both = lax.all_gather(w_both, 'tensor', axis=0)]
    pallas_call x0 -> x4, Pallas kernels: none -> 31.9 us  [sum_pairs(): pl.pallas_call(pair_kernel, out_shape=jax.ShapeDtypeStruct((n_out, rows,...]
    pallas_call x2, Pallas kernels: 75.4 us -> 106 us  [sum_over_data(): pl.pallas_call(functools.partial(sum_kernel, n), out_shape=jax.ShapeDtype...]
    reduce_scatter x4, waiting for transfers between devices: 27.8 us -> 53.1 us  [the longest x2 37.5 us: body(): lax.psum_scatter(partial_rows, 'tensor', scatter_dimension=0, axis_index_...]
    select_n x2, other arithmetic: 16 us -> 8.95 us  [body(): partial_rows = jnp.where(is_owned[:, None], picked, jnp.zeros_like(picked))]
    dot_general x4 -> x2, matrix products: 18.1 us -> 12.9 us  [the longest x1 7.74 us: body(): grad_w2 = lax.dot_general(hidden, d_out, TN, preferred_element_type=F32)]
    dot_general x2 -> x1, matrix products: 11.9 us -> 9.9 us  [body(): mlp_out = jnp.dot(hidden, w2, preferred_element_type=F32)]
  transfers between devices with their start and end apart: 6 -> 6, of which waited for: 5 -> 4; matrix products, arithmetic and copies ran while one was open for 16% -> 15% of each run, Pallas kernels for 19% -> 30%
where the time goes in v4:
time: 531 us; the launch traced here: 530 us
  Pallas kernels  251 us (47%)
  waiting for transfers between devices  99.8 us (19%)
  local copies, waits for them, and re-layouts  69.8 us (13%)
  matrix products  58.3 us (11%)
  other arithmetic  23.3 us (4%)
  between operations  15.7 us (3%)
  blocking collectives  11.5 us (2%)
    pallas_call x2, Pallas kernels, sum_over_data(): pl.pallas_call(functools.partial(sum_kernel, n), out_shape=jax.ShapeDtype...  106 us
    pallas_call x1, Pallas kernels, scatter_rows(): pl.pallas_call(functools.partial(scatter_kernel, rows.bit_length(), n_dev...  77.2 us
    gather x2, local copies, waits for them, and re-layouts, body(): picked = jnp.take(embed_table, jnp.where(is_owned, local_ids, 0), axis=0)  48.1 us
    reduce_scatter x2, waiting for transfers between devices, body(): lax.psum_scatter(partial_rows, 'tensor', scatter_dimension=0, axis_index_...  37.5 us
    pallas_call x1, Pallas kernels, list_owned(): pl.pallas_call(functools.partial(list_kernel, rows, bits, n_tok // n_part...  36.5 us
    all_gather x1, waiting for transfers between devices, body(): lax.all_gather(jnp.concatenate(grads, axis=0), ('data', 'tensor'), axis=0...  35.8 us
    pallas_call x4, Pallas kernels, sum_pairs(): pl.pallas_call(pair_kernel, out_shape=jax.ShapeDtypeStruct((n_out, rows,...  31.9 us
    dot_general x2, matrix products, body(): lax.dot_general(normed, w1t, NT, preferred_element_type=F32).astype(BF16)  20.2 us
  transfers between devices with their start and end apart: 6, of which 4 were waited for; matrix products, arithmetic and copies ran while one was open for 15% of the time, Pallas kernels for 30%

profile of v4, /device:TPU:97, one launch (start us, length us, event | category | flops | bytes accessed | tf_op | source)
XLA Modules:
  0.0 530.1 jit_solution(6670099387712838659)
XLA Ops:
  8.1 0.8 reshape.166
  9.0 28.5 %gather_fusion = bf16[5120,768]{1,0:T(8,128)(2,1)} fusion(bf16[6288,768]{1,0:T(8,128)(2,1)} %param.7, s32[5120]{0:T(1024)S(1)} %broadcast_clamp_fusion), kind=kCustom, calls=%fused_computation | custom fusion | bytes 15749120 | tf_op jit(solution)/shard_map/jit(_take)/gather | solution.py:268
  37.6 5.4 %select_select_fusion.blocks_ref = bf16[8,640,768]{2,1,0:T(8,128)(2,1)S(1)} fusion(bf16[8,640,768]{2,1,0:T(8,128)(2,1)} %bitcast.52, pred[8,640]{1,0:T(8,128)(4,1)S(1)} %get-tuple-element.26, pred[8,640]{1,0:T(8,128)(4,1)S(1)} %get-tuple-element.27), kind=kLoop, calls=%fused_computation.22 | loop fusion | flops 7864320 | bytes 15738880 | tf_op jit(solution)/shard_map/jit(_where)/select_n | solution.py:269
  42.9 8.9 %shard_map.93 = bf16[4,640,768]{2,1,0:T(8,128)(2,1)S(1)} custom-call(bf16[8,640,768]{2,1,0:T(8,128)(2,1)S(1)} %select_select_fusion.blocks_ref), custom_call_target="tpu_custom_call" | custom-call | flops 15728640000 | bytes 23592960 | tf_op jit(solution)/shard_map/pallas_call | solution.py:229
  51.8 2.0 copy-done.2
  54.2 0.7 copy-done.16
  54.9 1.1 pad_maximum_fusion.4
  56.2 19.5 %gather_fusion.1 = bf16[3072,768]{1,0:T(8,128)(2,1)} fusion(bf16[6288,768]{1,0:T(8,128)(2,1)} %param.7, s32[3072]{0:T(1024)S(1)} %broadcast_clamp_fusion.1), kind=kCustom, calls=%fused_computation.1 | custom fusion | bytes 9449472 | tf_op jit(solution)/shard_map/jit(_take)/gather | solution.py:268
  75.7 3.6 select_select_fusion.1.blocks_ref
  79.3 6.7 %shard_map.94 = bf16[4,384,768]{2,1,0:T(8,128)(2,1)} custom-call(bf16[8,384,768]{2,1,0:T(8,128)(2,1)S(1)} %select_select_fusion.1.blocks_ref), custom_call_target="tpu_custom_call" | custom-call | flops 9437184000 | bytes 14155776 | tf_op jit(solution)/shard_map/pallas_call | solution.py:229
  86.2 37.5 %reduce-scatter.5.cloned.1.call-done = bf16[640,768]{1,0:T(8,128)(2,1)} async-done(((bf16[2560,768]{1,0:T(8,128)(2,1)}), bf16[640,768]{1,0:T(8,128)(2,1)}) %reduce-scatter.5.cloned.1.call-update) | async-done | bytes 983056 | tf_op jit(solution)/shard_map/reduce_scatter | solution.py:272
  123.7 1.5 fusion.29
  125.1 1.5 fusion.23
  126.6 10.6 %all-gather.7.cloned.1.call-done = bf16[6144,768]{1,0:T(8,128)(2,1)} async-done(((bf16[768,768]{1,0:T(8,128)(2,1)}), bf16[6144,768]{1,0:T(8,128)(2,1)}) %all-gather.7.cloned.1.call-update) | async-done | bytes 9437200 | tf_op jit(solution)/shard_map/all_gather | solution.py:256
  137.2 6.9 %fusion.44 = (bf16[8,384,768]{2,1,0:T(8,128)(2,1)S(1)}, bf16[8,384,768]{2,1,0:T(8,128)(2,1)}) fusion(bf16[8,768,768]{2,1,0:T(8,128)(2,1)} %bitcast.54), kind=kLoop, calls=%fused_computation.91 | loop fusion | bytes 18874368 | tf_op jit(solution)/shard_map/slice | solution.py:258
  144.1 5.6 %convolution_bitcast_fusion = f32[640,3072]{1,0:T(8,128)} fusion(bf16[3072,768]{1,0:T(8,128)(2,1)S(1)} %bitcast.55, bf16[1024,768]{1,0:T(8,128)(2,1)S(1)} %copy-done.14), kind=kOutput, calls=%fused_computation.26 | convolution fusion | flops 3019898880 | bytes 13565952 | tf_op jit(solution)/shard_map/dot_general | solution.py:281
  149.9 11.3 %fusion.7 = (bf16[640,3072]{1,0:T(8,128)(2,1)}, bf16[640,3072]{1,0:T(8,128)(2,1)S(1)}) fusion(f32[640,3072]{1,0:T(8,128)} %convolution_bitcast_fusion, bf16[640,768]{1,0:T(8,128)(2,1)S(1)} %fusion.23, bf16[3072,768]{1,0:T(8,128)(2,1)S(1)} %bitcast.59), kind=kOutput, calls=%fused_computation.19 | convolution fusion | flops 3067084800 | bytes 21430272 | tf_op jit(solution)/shard_map/dot_general | solution.py:290
  161.2 3.4 fusion.24
  164.5 0.6 fusion.28
  165.2 4.2 convolution_bitcast_fusion.1
  169.4 1.4 fusion.39
  170.9 1.3 fusion.33
  172.2 8.9 %fusion.13 = (bf16[384,3072]{1,0:T(8,128)(2,1)S(1)}, bf16[384,3072]{1,0:T(8,128)(2,1)S(1)}) fusion(f32[384,3072]{1,0:T(8,128)} %convolution_bitcast_fusion.1, bf16[384,768]{1,0:T(8,128)(2,1)S(1)} %fusion.33, bf16[3072,768]{1,0:T(8,128)(2,1)} %bitcast.58), kind=kOutput, calls=%fused_computation.30 | convolution fusion | flops 1840250880 | bytes 14745600 | tf_op jit(solution)/shard_map/dot_general | solution.py:290
  181.2 2.1 fusion.34
  183.3 1.6 fusion.38
  185.0 0.6 copy-done.9
  185.7 3.5 pad_maximum_fusion
  189.2 5.2 fusion.45
  194.4 8.2 %shard_map.97 = f32[4,384,768]{2,1,0:T(8,128)S(1)} custom-call(f32[8,384,768]{2,1,0:T(8,128)S(1)} %bitcast.50), custom_call_target="tpu_custom_call" | custom-call | flops 9437184000 | bytes 14155776 | tf_op jit(solution)/shard_map/pallas_call | solution.py:229
  202.6 2.1 copy-done
  204.8 7.7 %fusion.46 = f32[3072,768]{1,0:T(8,128)S(1)} fusion(bf16[1024,3072]{1,0:T(8,128)(2,1)} %get-tuple-element.40, bf16[1024,768]{1,0:T(8,128)(2,1)} %param.11), kind=kOutput, calls=%fused_computation.93 | convolution fusion | flops 4831838208 | bytes 17301504 | tf_op jit(solution)/shard_map/dot_general | solution.py:307
  212.6 8.2 %shard_map.99 = f32[4,384,768]{2,1,0:T(8,128)S(1)} custom-call(f32[8,384,768]{2,1,0:T(8,128)S(1)} %bitcast.51), custom_call_target="tpu_custom_call" | custom-call | flops 9437184000 | bytes 14155776 | tf_op jit(solution)/shard_map/pallas_call | solution.py:229
  220.8 2.2 copy-done.1
  223.2 1.2 pad_maximum_fusion.2
  224.5 36.5 %shard_map.95 = s32[8320]{0:T(1024)} custom-call(s32[1]{0:T(128)} %bitcast.12.base_ref, s32[8192]{0:T(1024)} %ids_ref.1), custom_call_target="tpu_custom_call" | custom-call | flops 32768000 | bytes 65536 | tf_op jit(solution)/shard_map/pallas_call | solution.py:46
  261.0 0.8 reshape.192
  261.8 11.5 %all-gather.1 = s32[4,1,8320]{2,1,0:T(1,128)S(1)} all-gather(s32[1,1,8320]{2,1,0:T(1,128)S(1)} %reshape.192), channel_id=1, replica_groups=mesh['pod'=1,'data'=4,'tensor'=8] {'data'}, dimensions={0}, use_global_device_ids=true | all-gather | bytes 166400 | tf_op jit(solution)/shard_map/all_gather | solution.py:276
  273.2 0.3 reduce
  273.7 9.9 %add_convert_fusion = bf16[1024,768]{1,0:T(8,128)(2,1)} fusion(bf16[1024,3072]{1,0:T(8,128)(2,1)} %get-tuple-element.40, bf16[3072,768]{1,0:T(8,128)(2,1)} %bitcast.57, bf16[384,768]{1,0:T(8,128)(2,1)S(1)} %copy-done.6, bf16[640,768]{1,0:T(8,128)(2,1)S(1)} %copy-done.5), kind=kOutput, calls=%fused_computation.40 | convolution fusion | flops 4836556800 | bytes 14155776 | tf_op jit(solution)/shard_map/dot_general | solution.py:303
  283.6 1.3 copy-done.3
  284.9 47.5 %shard_map.98 = f32[384,768]{1,0:T(8,128)S(1)} custom-call(f32[384,768]{1,0:T(8,128)S(1)} %copy-done.3), custom_call_target="tpu_custom_call" | custom-call | flops 14745600000 | bytes 2359296 | tf_op jit(solution)/shard_map/pallas_call | solution.py:172
  332.4 1.4 copy.17
  333.8 15.6 %reduce-scatter.11.cloned.1.call-done.part_ref = f32[384,768]{1,0:T(8,128)} async-done(((f32[1536,768]{1,0:T(8,128)}), f32[384,768]{1,0:T(8,128)}) %reduce-scatter.11.cloned.1.call-update) | async-done | bytes 1179664 | tf_op jit(solution)/shard_map/reduce_scatter | solution.py:311
  349.4 1.3 copy-done.4
  350.7 58.3 %shard_map.100 = f32[384,768]{1,0:T(8,128)S(1)} custom-call(f32[384,768]{1,0:T(8,128)S(1)} %copy-done.4), custom_call_target="tpu_custom_call" | custom-call | flops 14745600000 | bytes 2359296 | tf_op jit(solution)/shard_map/pallas_call | solution.py:172
  409.0 35.8 %all-gather.5.cloned.1.call-done.part_ref = bf16[32768,768]{1,0:T(8,128)(2,1)} async-done(((bf16[1024,768]{1,0:T(8,128)(2,1)}), bf16[32768,768]{1,0:T(8,128)(2,1)}) %all-gather.5.cloned.1.call-update) | async-done | bytes 50331664 | tf_op jit(solution)/shard_map/all_gather | solution.py:305
  444.8 77.2 %shard_map.96 = f32[6288,768]{1,0:T(8,128)} custom-call(s32[33280]{0:T(1024)S(1)} %reshape.193.list_ref, bf16[32768,768]{1,0:T(8,128)(2,1)} %all-gather.5.cloned.1.call-done.part_ref), custom_call_target="tpu_custom_call" | custom-call | flops 32768000000 | bytes 69648384 | tf_op jit(solution)/shard_map/pallas_call | solution.py:110
  522.0 1.0 copy.23
  (66 shorter events, 1.6 us)
Async XLA Ops:
  8.0 115.6 %reduce-scatter.5.cloned.1.call-start = ((), (), s32[]{:S(2)}) async-start(), calls=%async_computation.4 | async-start | bytes 4915200 | tf_op jit(solution)/shard_map/reduce_scatter | solution.py:272
  42.9 11.0 %copy-start.15 = (bf16[768,384]{1,0:T(8,128)(2,1)S(1)}, bf16[768,384]{1,0:T(8,128)(2,1)}, u32[]{:S(2)}) copy-start(bf16[768,384]{1,0:T(8,128)(2,1)} %param.9) | copy-start | bytes 1769476
  51.8 2.0 copy-start.2
  53.8 1.1 copy-start.16
  53.9 83.3 %all-gather.7.cloned.1.call-start = ((), (), s32[]{:S(2)}) async-start(), calls=%async_computation.9 | async-start | bytes 10616832 | tf_op jit(solution)/shard_map/all_gather | solution.py:256
  56.0 113.4 %reduce-scatter.7.cloned.1.call-start = ((), (), s32[]{:S(2)}) async-start(), calls=%async_computation.5 | async-start | bytes 2949120 | tf_op jit(solution)/shard_map/reduce_scatter | solution.py:272
  79.3 6.8 %copy-start.17 = (bf16[768]{0:T(1024)(128)(2,1)S(1)}, bf16[768]{0:T(1024)(128)(2,1)}, u32[]{:S(2)}) copy-start(bf16[768]{0:T(1024)(128)(2,1)} %param.8) | copy-start | bytes 4612
  86.1 197.5 %reduce-scatter.9.cloned.1.call-start = ((), (), s32[]{:S(2)}) async-start(), calls=%async_computation.7 | async-start | bytes 5898240 | tf_op jit(solution)/shard_map/reduce_scatter | solution.py:312
  126.6 23.1 %copy-start.12 = (bf16[640,768]{1,0:T(8,128)(2,1)}, bf16[640,768]{1,0:T(8,128)(2,1)S(1)}, u32[]{:S(2)}) copy-start(bf16[640,768]{1,0:T(8,128)(2,1)S(1)} %fusion.23) | copy-start | bytes 2949124
  137.2 6.9 %copy-start.14 = (bf16[1024,768]{1,0:T(8,128)(2,1)S(1)}, bf16[1024,768]{1,0:T(8,128)(2,1)}, u32[]{:S(2)}) copy-start(bf16[1024,768]{1,0:T(8,128)(2,1)} %param.11) | copy-start | bytes 4718596
  144.1 21.1 %copy-start.7 = (bf16[8,384,768]{2,1,0:T(8,128)(2,1)}, bf16[8,384,768]{2,1,0:T(8,128)(2,1)S(1)}, u32[]{:S(2)}) copy-start(bf16[8,384,768]{2,1,0:T(8,128)(2,1)S(1)} %get-tuple-element.30) | copy-start | bytes 14155780
  144.1 5.7 %copy-start.8 = (bf16[8,384,768]{2,1,0:T(8,128)(2,1)S(1)}, bf16[8,384,768]{2,1,0:T(8,128)(2,1)}, u32[]{:S(2)}) copy-start(bf16[8,384,768]{2,1,0:T(8,128)(2,1)} %get-tuple-element.31) | copy-start | bytes 14155780
  149.9 11.3 %copy-start.5 = (bf16[640,768]{1,0:T(8,128)(2,1)S(1)}, bf16[640,768]{1,0:T(8,128)(2,1)}, u32[]{:S(2)}) copy-start(bf16[640,768]{1,0:T(8,128)(2,1)} %reduce-scatter.5.cloned.1.call-done) | copy-start | bytes 2949124
  161.2 3.4 copy-start.10
  169.4 11.7 %slice-start = ((s8[4718592]{0:T(1024)(128)(4,1)}), s8[4194304]{0:T(1024)(128)(4,1)S(1)}, s32[]{:S(2)}) async-start(s8[4718592]{0:T(1024)(128)(4,1)} %bitcast.61), calls=%async_computation.10 | async-start | bytes 8388608
  172.1 9.0 %copy-start.6 = (bf16[384,768]{1,0:T(8,128)(2,1)S(1)}, bf16[384,768]{1,0:T(8,128)(2,1)}, u32[]{:S(2)}) copy-start(bf16[384,768]{1,0:T(8,128)(2,1)} %reduce-scatter.7.cloned.1.call-done) | copy-start | bytes 1769476
  172.2 9.0 %slice-start.1 = ((s8[4718592]{0:T(1024)(128)(4,1)}), s8[524288]{0:T(1024)(128)(4,1)S(1)}, s32[]{:S(2)}) async-start(s8[4718592]{0:T(1024)(128)(4,1)} %bitcast.61), calls=%async_computation.11 | async-start | bytes 1048576
  181.2 3.7 copy-start.13
  181.2 3.9 copy-start.11
  183.3 2.4 copy-start.9
  202.6 2.1 copy-start
  204.8 144.6 %reduce-scatter.11.cloned.1.call-start = ((), (), s32[]{:S(2)}) async-start(), calls=%async_computation.8 | async-start | bytes 5898240 | tf_op jit(solution)/shard_map/reduce_scatter | solution.py:311
  220.8 2.2 copy-start.1
  223.1 221.7 %all-gather.5.cloned.1.call-start = ((), (), s32[]{:S(2)}) async-start(), calls=%async_computation.6 | async-start | bytes 51904512 | tf_op jit(solution)/shard_map/all_gather | solution.py:305
  283.6 1.3 copy-start.3
  349.4 1.3 copy-start.4
Sparse Core Ops, SparseCore 0:
  54.0 69.6 reduce-scatter.4
  126.0 29.3 reduce-scatter.6
  204.9 55.9 reduce-scatter.8
  263.1 86.2 reduce-scatter.10
Sparse Core Ops, SparseCore 1:
  56.5 80.6 all-gather.6
  225.7 219.0 all-gather.4
